TPU v7x, 32 devices: a whole 2x2x4 slice. The times are simulated.
32 devices in a mesh: srow: 4 (over y, core), scol: 8 (over z, x).
Axes of the slice: x: 2, y: 2, z: 4, core: 2. Of those that a mesh axis runs over, the one named last changes fastest.
Arguments:
- loads: float32 [4, 16, 4, 128], P('srow', 'scol'), may hold values from -6 to 6
- local_inverse: float32 [4, 16, 128, 128], P('srow', 'scol'), as said below
- dirichlet: float32 [4, 16, 128, 128], P('srow', 'scol'), as said below
- corner_coupling: float32 [4, 16, 128], P('srow', 'scol'), may hold values from -4 to 4
- coarse_inverse: float32 [4, 16, 16], P('srow', 'scol'), as said below
- partner: int32 [4, 16, 128], P('srow', 'scol'), may hold values from -1 to 31, as said below
Outputs:
- multipliers: float32 [4, 16, 4, 128], P('srow', 'scol')
- residual: float32 [4, 16, 4, 128], P('srow', 'scol')
Inputs may be any that keep to these rules, and one draw needn't show every extreme that they name: `partner`: on each edge of each subdomain the first n entries, for some n of 1 to 32, are the positions 0 to n - 1 in order or reversed, the rest are -1; the two subdomains sharing an edge have the same n and mutually inverse lists. `local_inverse`: each block is symmetric positive definite. `dirichlet`: each block is symmetric positive definite. `coarse_inverse`: each band's matrix is symmetric positive definite.
All inputs are finite; a program needn't handle non-finite values.
Results may differ from a plain program's by a relative error of at most 0.0003.
Values sent between devices are 32-bit elements; how exact they have to be, the bound alone decides.
A program may use at most 64 MiB of HBM per device.

v0:
```python
import jax
import jax.numpy as jnp
from jax import lax
from jax.sharding import PartitionSpec as P

ITERS = 3
precise = lax.Precision.HIGHEST


def with_halo(cells, sides, width):
    for axis, dim in sides:
        count = lax.axis_size(axis)
        head = lax.slice_in_dim(cells, 0, width, axis=dim)
        tail = lax.slice_in_dim(cells, cells.shape[dim] - width, cells.shape[dim], axis=dim)
        cells = jnp.concatenate(
            [
                lax.ppermute(tail, axis, [(i, (i + 1) % count) for i in range(count)]),
                cells,
                lax.ppermute(head, axis, [((i + 1) % count, i) for i in range(count)]),
            ],
            axis=dim,
        )
    return cells


def facing_edges(values):
    edge_len = values.shape[-1] // 4
    sideways = with_halo(values[..., 0 : 2 * edge_len], (("scol", 1),), 1)
    vertical = with_halo(values[..., 2 * edge_len :], (("srow", 0),), 1)
    west_side = sideways[:, :-2, :, edge_len : 2 * edge_len]
    east_side = sideways[:, 2:, :, 0:edge_len]
    south_side = vertical[:-2, :, :, edge_len : 2 * edge_len]
    north_side = vertical[2:, :, :, 0:edge_len]
    return jnp.concatenate([west_side, east_side, south_side, north_side], axis=-1)


def jump(values, partner):
    edge_len = values.shape[-1] // 4
    facing = facing_edges(values)
    offset = jnp.arange(values.shape[-1], dtype=jnp.int32) // edge_len * edge_len
    position = jnp.clip(partner, 0, edge_len - 1) + offset
    position = jnp.broadcast_to(position[:, :, None, :], values.shape)
    picked = jnp.take_along_axis(facing, position, axis=-1)
    return jnp.where(partner[:, :, None, :] >= 0, values - picked, jnp.zeros_like(values))


def apply_inverse(values, local_inverse, corner_coupling, coarse_inverse):
    sub_rows, sub_cols, rhs_count, width = values.shape
    blocks = jnp.einsum("ijab,ijrb->ijra", local_inverse, values, precision=precise)
    coarse_in = jnp.einsum("ijb,ijrb->ijr", corner_coupling, values, precision=precise)
    coarse_in = coarse_in.reshape(sub_rows * sub_cols, rhs_count)
    band_rows = coarse_inverse[0]
    coarse_out = jnp.dot(
        band_rows,
        lax.all_gather(coarse_in, "scol", axis=0, tiled=True),
        precision=precise,
        preferred_element_type=jnp.float32,
    )
    coarse_out = coarse_out.reshape(sub_rows, sub_cols, rhs_count)
    return blocks + corner_coupling[:, :, None, :] * coarse_out[..., None]


def inner(left, right):
    return jnp.sum(left * right, axis=(0, 1, 3))


def global_sums(first_dot, second_dot):
    return lax.psum((first_dot, second_dot), ("srow", "scol"))


def scaled(coef, values):
    return coef[None, None, :, None] * values


def body(loads, local_inverse, dirichlet, corner_coupling, coarse_inverse, partner):

    def operator(values):
        spread = jump(values, partner)
        return jump(apply_inverse(spread, local_inverse, corner_coupling, coarse_inverse), partner)

    def precond(values):
        spread = jump(values, partner)
        return jump(jnp.einsum("ijab,ijrb->ijra", dirichlet, spread, precision=precise), partner)

    right = operator(loads)
    multipliers = jnp.zeros_like(right)
    residual = right
    precon = precond(residual)
    image = operator(precon)
    gamma, curvature = global_sums(inner(residual, precon), inner(precon, image))
    step_size = gamma / curvature
    search = precon
    along = image
    for iteration in range(ITERS):
        multipliers = multipliers + scaled(step_size, search)
        residual = residual - scaled(step_size, along)
        if iteration + 1 < ITERS:
            precon = precond(residual)
            image = operator(precon)
            gamma_new, curvature = global_sums(inner(residual, precon), inner(precon, image))
            dir_ratio = gamma_new / gamma
            step_size = gamma_new / (curvature - dir_ratio * gamma_new / step_size)
            search = precon + scaled(dir_ratio, search)
            along = image + scaled(dir_ratio, along)
            gamma = gamma_new
    return (multipliers, residual)


def solution(mesh):
    return jax.shard_map(
        body,
        mesh=mesh,
        in_specs=(
            P("srow", "scol", None, None),
            P("srow", "scol", None, None),
            P("srow", "scol", None, None),
            P("srow", "scol", None),
            P("srow", "scol", None),
            P("srow", "scol", None),
        ),
        out_specs=(P("srow", "scol", None, None), P("srow", "scol", None, None)),
        check_vma=False,
    )
```

profile of v0, /device:TPU:0, one launch (start us, length us, event | category | flops | bytes accessed | tf_op | source)
XLA Modules:
  0.0 464.1 jit_solution(16173901481340105120)
XLA Ops:
  2.0 1.9 collective-permute-start.3
  4.0 2.3 collective-permute-start
  6.2 3.1 collective-permute-start.1
  10.9 9.6 %gather_fusion = f32[1024]{0:T(1024)S(1)} fusion(f32[2,4,128]{2,1,0:T(4,128)S(1)} %fusion.69, s32[1024]{0:T(1024)S(1)} %bitcast.196), kind=kCustom, calls=%fused_computation.clone | custom fusion | bytes 20480 | tf_op jit(solution)/shard_map/jit(take_along_axis)/gather | solution.py:43
  21.3 21.1 %all-gather = f32[8,2,4]{2,1,0:T(2,128)S(1)} all-gather(f32[1,2,4]{2,1,0:T(2,128)S(1)} %bitcast.256), channel_id=1, replica_groups=mesh['srow'=4,'scol'=8] {'scol'}, dimensions={0}, use_global_device_ids=true | all-gather | bytes 288 | tf_op jit(solution)/shard_map/all_gather | solution.py:55
  43.6 1.7 collective-permute-start.7
  45.4 4.7 %collective-permute-start.5 = (f32[1,1,4,64]{3,2,1,0:T(4,128)S(1)}, f32[1,1,4,64]{3,2,1,0:T(4,128)S(1)}, u32[]{:S(2)}, u32[]{:S(2)}) collective-permute-start(f32[1,1,4,64]{3,2,1,0:T(4,128)S(1)} %get-tuple-element.76), channel_id=1, source_target_pairs={{1,0},{2,1},{3,2},{4,3},{5,4},{6,5},{7,6},{0,7},{9,8},{10,9},{11,1... | collective-permute-start | bytes 3080 | tf_op jit(solution)/shard_map/ppermute | solution.py:19
  50.2 1.5 collective-permute-done.4
  51.7 9.6 %gather_fusion.1 = f32[1024]{0:T(1024)S(1)} fusion(f32[2,4,128]{2,1,0:T(4,128)S(1)} %fusion.65, s32[1024]{0:T(1024)S(1)} %bitcast.197), kind=kCustom, calls=%fused_computation.1.clone | custom fusion | bytes 20480 | tf_op jit(solution)/shard_map/jit(take_along_axis)/gather | solution.py:43
  61.5 1.7 collective-permute-start.11
  63.2 4.7 %collective-permute-start.9 = (f32[1,1,4,64]{3,2,1,0:T(4,128)S(1)}, f32[1,1,4,64]{3,2,1,0:T(4,128)S(1)}, u32[]{:S(2)}, u32[]{:S(2)}) collective-permute-start(f32[1,1,4,64]{3,2,1,0:T(4,128)S(1)} %get-tuple-element.72), channel_id=1, source_target_pairs={{1,0},{2,1},{3,2},{4,3},{5,4},{6,5},{7,6},{0,7},{9,8},{10,9},{11,1... | collective-permute-start | bytes 3080 | tf_op jit(solution)/shard_map/ppermute | solution.py:19
  68.0 1.5 collective-permute-done.8
  69.6 9.6 %gather_fusion.2 = f32[1024]{0:T(1024)S(1)} fusion(f32[2,4,128]{2,1,0:T(4,128)S(1)} %fusion.61, s32[1024]{0:T(1024)S(1)} %bitcast.198), kind=kCustom, calls=%fused_computation.2.clone | custom fusion | bytes 20480 | tf_op jit(solution)/shard_map/jit(take_along_axis)/gather | solution.py:43
  79.6 1.8 collective-permute-start.15
  81.3 4.7 %collective-permute-start.13 = (f32[1,1,4,64]{3,2,1,0:T(4,128)S(1)}, f32[1,1,4,64]{3,2,1,0:T(4,128)S(1)}, u32[]{:S(2)}, u32[]{:S(2)}) collective-permute-start(f32[1,1,4,64]{3,2,1,0:T(4,128)S(1)} %get-tuple-element.68), channel_id=1, source_target_pairs={{1,0},{2,1},{3,2},{4,3},{5,4},{6,5},{7,6},{0,7},{9,8},{10,9},{11,1... | collective-permute-start | bytes 3080 | tf_op jit(solution)/shard_map/ppermute | solution.py:19
  86.1 1.5 collective-permute-done.12
  87.7 9.6 %gather_fusion.3 = f32[1024]{0:T(1024)S(1)} fusion(f32[2,4,128]{2,1,0:T(4,128)S(1)} %fusion.57, s32[1024]{0:T(1024)S(1)} %bitcast.199), kind=kCustom, calls=%fused_computation.3.clone | custom fusion | bytes 20480 | tf_op jit(solution)/shard_map/jit(take_along_axis)/gather | solution.py:43
  97.4 1.7 collective-permute-start.19
  99.2 4.7 %collective-permute-start.17 = (f32[1,1,4,64]{3,2,1,0:T(4,128)S(1)}, f32[1,1,4,64]{3,2,1,0:T(4,128)S(1)}, u32[]{:S(2)}, u32[]{:S(2)}) collective-permute-start(f32[1,1,4,64]{3,2,1,0:T(4,128)S(1)} %get-tuple-element.64), channel_id=1, source_target_pairs={{1,0},{2,1},{3,2},{4,3},{5,4},{6,5},{7,6},{0,7},{9,8},{10,9},{11,1... | collective-permute-start | bytes 3080 | tf_op jit(solution)/shard_map/ppermute | solution.py:19
  104.0 1.5 collective-permute-done.16
  105.5 9.6 %gather_fusion.4 = f32[1024]{0:T(1024)S(1)} fusion(f32[2,4,128]{2,1,0:T(4,128)S(1)} %fusion.53, s32[1024]{0:T(1024)S(1)} %bitcast.200), kind=kCustom, calls=%fused_computation.4.clone | custom fusion | bytes 20480 | tf_op jit(solution)/shard_map/jit(take_along_axis)/gather | solution.py:43
  115.3 21.0 %all-gather.1 = f32[8,2,4]{2,1,0:T(2,128)S(1)} all-gather(f32[1,2,4]{2,1,0:T(2,128)S(1)} %bitcast.257), channel_id=1, replica_groups=mesh['srow'=4,'scol'=8] {'scol'}, dimensions={0}, use_global_device_ids=true | all-gather | bytes 288 | tf_op jit(solution)/shard_map/all_gather | solution.py:55
  136.8 1.7 collective-permute-start.23
  138.6 4.7 %collective-permute-start.21 = (f32[1,1,4,64]{3,2,1,0:T(4,128)S(1)}, f32[1,1,4,64]{3,2,1,0:T(4,128)S(1)}, u32[]{:S(2)}, u32[]{:S(2)}) collective-permute-start(f32[1,1,4,64]{3,2,1,0:T(4,128)S(1)} %get-tuple-element.60), channel_id=1, source_target_pairs={{1,0},{2,1},{3,2},{4,3},{5,4},{6,5},{7,6},{0,7},{9,8},{10,9},{11,1... | collective-permute-start | bytes 3080 | tf_op jit(solution)/shard_map/ppermute | solution.py:19
  143.4 1.5 collective-permute-done.20
  144.9 9.6 %gather_fusion.5 = f32[1024]{0:T(1024)S(1)} fusion(f32[2,4,128]{2,1,0:T(4,128)S(1)} %fusion.49, s32[1024]{0:T(1024)S(1)} %bitcast.201), kind=kCustom, calls=%fused_computation.5.clone | custom fusion | bytes 20480 | tf_op jit(solution)/shard_map/jit(take_along_axis)/gather | solution.py:43
  154.7 40.2 %all-reduce.2 = (f32[4]{0:T(128)S(1)}, f32[4]{0:T(128)S(1)}) all-reduce(f32[4]{0:T(128)S(1)} %get-tuple-element.8, f32[4]{0:T(128)S(1)} %get-tuple-element.7), channel_id=1, replica_groups=mesh['srow'=4,'scol'=8] {'srow','scol'}, use_global_device_ids=true, to_apply=%region_1.3 | all-reduce | flops 8 | bytes 64 | tf_op jit(solution)/shard_map/psum | solution.py:68
  195.1 1.7 collective-permute-start.27
  196.8 2.3 collective-permute-start.24
  199.1 2.4 collective-permute-start.25
  201.6 1.5 collective-permute-done.24
  203.2 9.6 %gather_fusion.6 = f32[1024]{0:T(1024)S(1)} fusion(f32[2,4,128]{2,1,0:T(4,128)S(1)} %fusion.45, s32[1024]{0:T(1024)S(1)} %bitcast.202), kind=kCustom, calls=%fused_computation.6.clone | custom fusion | bytes 20480 | tf_op jit(solution)/shard_map/jit(take_along_axis)/gather | solution.py:43
  213.2 1.8 collective-permute-start.31
  214.9 1.8 collective-permute-start.28
  216.7 2.9 collective-permute-start.29
  219.7 1.5 collective-permute-done.28
  221.3 9.6 %gather_fusion.7 = f32[1024]{0:T(1024)S(1)} fusion(f32[2,4,128]{2,1,0:T(4,128)S(1)} %fusion.41, s32[1024]{0:T(1024)S(1)} %bitcast.203), kind=kCustom, calls=%fused_computation.7.clone | custom fusion | bytes 20480 | tf_op jit(solution)/shard_map/jit(take_along_axis)/gather | solution.py:43
  231.0 1.7 collective-permute-start.35
  234.1 3.4 collective-permute-start.33
  237.6 1.5 collective-permute-done.32
  239.1 9.6 %gather_fusion.8 = f32[1024]{0:T(1024)S(1)} fusion(f32[2,4,128]{2,1,0:T(4,128)S(1)} %fusion.37, s32[1024]{0:T(1024)S(1)} %bitcast.204), kind=kCustom, calls=%fused_computation.8.clone | custom fusion | bytes 20480 | tf_op jit(solution)/shard_map/jit(take_along_axis)/gather | solution.py:43
  248.9 21.0 %all-gather.2 = f32[8,2,4]{2,1,0:T(2,128)S(1)} all-gather(f32[1,2,4]{2,1,0:T(2,128)S(1)} %bitcast.258), channel_id=1, replica_groups=mesh['srow'=4,'scol'=8] {'scol'}, dimensions={0}, use_global_device_ids=true | all-gather | bytes 288 | tf_op jit(solution)/shard_map/all_gather | solution.py:55
  270.4 1.7 collective-permute-start.39
  272.2 4.7 %collective-permute-start.37 = (f32[1,1,4,64]{3,2,1,0:T(4,128)S(1)}, f32[1,1,4,64]{3,2,1,0:T(4,128)S(1)}, u32[]{:S(2)}, u32[]{:S(2)}) collective-permute-start(f32[1,1,4,64]{3,2,1,0:T(4,128)S(1)} %get-tuple-element.44), channel_id=1, source_target_pairs={{1,0},{2,1},{3,2},{4,3},{5,4},{6,5},{7,6},{0,7},{9,8},{10,9},{11,1... | collective-permute-start | bytes 3080 | tf_op jit(solution)/shard_map/ppermute | solution.py:19
  278.5 9.6 %gather_fusion.9 = f32[1024]{0:T(1024)S(1)} fusion(f32[2,4,128]{2,1,0:T(4,128)S(1)} %fusion.33, s32[1024]{0:T(1024)S(1)} %bitcast.205), kind=kCustom, calls=%fused_computation.9.clone | custom fusion | bytes 20480 | tf_op jit(solution)/shard_map/jit(take_along_axis)/gather | solution.py:43
  288.3 40.8 %all-reduce.1 = (f32[4]{0:T(128)S(1)}, f32[4]{0:T(128)S(1)}) all-reduce(f32[4]{0:T(128)S(1)} %get-tuple-element.6, f32[4]{0:T(128)S(1)} %get-tuple-element.5), channel_id=1, replica_groups=mesh['srow'=4,'scol'=8] {'srow','scol'}, use_global_device_ids=true, to_apply=%region_5.7 | all-reduce | flops 8 | bytes 64 | tf_op jit(solution)/shard_map/psum | solution.py:68
  329.3 1.8 collective-permute-start.43
  331.1 2.3 collective-permute-start.40
  333.3 2.4 collective-permute-start.41
  337.4 9.6 %gather_fusion.10 = f32[1024]{0:T(1024)S(1)} fusion(f32[2,4,128]{2,1,0:T(4,128)S(1)} %fusion.29, s32[1024]{0:T(1024)S(1)} %bitcast.206), kind=kCustom, calls=%fused_computation.10.clone | custom fusion | bytes 20480 | tf_op jit(solution)/shard_map/jit(take_along_axis)/gather | solution.py:43
  347.4 1.8 collective-permute-start.47
  349.2 1.8 collective-permute-start.44
  351.0 2.9 collective-permute-start.45
  354.0 1.5 collective-permute-done.44
  355.5 9.6 %gather_fusion.11 = f32[1024]{0:T(1024)S(1)} fusion(f32[2,4,128]{2,1,0:T(4,128)S(1)} %fusion.25, s32[1024]{0:T(1024)S(1)} %bitcast.207), kind=kCustom, calls=%fused_computation.11.clone | custom fusion | bytes 20480 | tf_op jit(solution)/shard_map/jit(take_along_axis)/gather | solution.py:43
  365.3 1.7 collective-permute-start.51
  368.4 3.4 collective-permute-start.49
  371.8 1.5 collective-permute-done.48
  373.4 9.6 %gather_fusion.12 = f32[1024]{0:T(1024)S(1)} fusion(f32[2,4,128]{2,1,0:T(4,128)S(1)} %fusion.21, s32[1024]{0:T(1024)S(1)} %bitcast.208), kind=kCustom, calls=%fused_computation.12.clone | custom fusion | bytes 20480 | tf_op jit(solution)/shard_map/jit(take_along_axis)/gather | solution.py:43
  383.1 21.0 %all-gather.3 = f32[8,2,4]{2,1,0:T(2,128)S(1)} all-gather(f32[1,2,4]{2,1,0:T(2,128)S(1)} %bitcast.259), channel_id=1, replica_groups=mesh['srow'=4,'scol'=8] {'scol'}, dimensions={0}, use_global_device_ids=true | all-gather | bytes 288 | tf_op jit(solution)/shard_map/all_gather | solution.py:55
  404.7 1.7 collective-permute-start.55
  406.4 4.7 %collective-permute-start.53 = (f32[1,1,4,64]{3,2,1,0:T(4,128)S(1)}, f32[1,1,4,64]{3,2,1,0:T(4,128)S(1)}, u32[]{:S(2)}, u32[]{:S(2)}) collective-permute-start(f32[1,1,4,64]{3,2,1,0:T(4,128)S(1)} %get-tuple-element.28), channel_id=1, source_target_pairs={{1,0},{2,1},{3,2},{4,3},{5,4},{6,5},{7,6},{0,7},{9,8},{10,9},{11,1... | collective-permute-start | bytes 3080 | tf_op jit(solution)/shard_map/ppermute | solution.py:19
  412.8 9.6 %gather_fusion.13 = f32[1024]{0:T(1024)S(1)} fusion(f32[2,4,128]{2,1,0:T(4,128)S(1)} %fusion.17, s32[1024]{0:T(1024)S(1)} %bitcast.209), kind=kCustom, calls=%fused_computation.13.clone | custom fusion | bytes 20480 | tf_op jit(solution)/shard_map/jit(take_along_axis)/gather | solution.py:43
  422.5 40.8 %all-reduce = (f32[4]{0:T(128)S(1)}, f32[4]{0:T(128)S(1)}) all-reduce(f32[4]{0:T(128)S(1)} %get-tuple-element.4, f32[4]{0:T(128)S(1)} %get-tuple-element.3), channel_id=1, replica_groups=mesh['srow'=4,'scol'=8] {'srow','scol'}, use_global_device_ids=true, to_apply=%region_9.11 | all-reduce | flops 8 | bytes 64 | tf_op jit(solution)/shard_map/psum | solution.py:68
  (171 shorter events, 19.1 us)
Async XLA Ops:
  0.6 42.6 %copy-start = (f32[1,2,128,128]{3,2,1,0:T(8,128)S(1)}, f32[1,2,128,128]{3,2,1,0:T(8,128)}, u32[]{:S(2)}) copy-start(f32[1,2,128,128]{3,2,1,0:T(8,128)} %param.9) | copy-start | bytes 393220
  0.6 3.3 copy-start.2
  1.5 7.9 %collective-permute-start.2 = (f32[1,2,4,64]{3,2,1,0:T(4,128)S(1)}, f32[1,2,4,64]{3,2,1,0:T(4,128)S(1)}, u32[]{:S(2)}, u32[]{:S(2)}) collective-permute-start(f32[1,2,4,64]{3,2,1,0:T(4,128)S(1)} %get-tuple-element.77), channel_id=1, source_target_pairs={{0,8},{8,16},{16,24},{24,0},{1,9},{9,17},{17,25},{25,1},{2,10},{10... | collective-permute-start | bytes 6152 | tf_op jit(solution)/shard_map/ppermute | solution.py:17
  2.0 8.8 %collective-permute-start.3 = (f32[1,2,4,64]{3,2,1,0:T(4,128)S(1)}, f32[1,2,4,64]{3,2,1,0:T(4,128)S(1)}, u32[]{:S(2)}, u32[]{:S(2)}) collective-permute-start(f32[1,2,4,64]{3,2,1,0:T(4,128)S(1)} %get-tuple-element.77), channel_id=1, source_target_pairs={{8,0},{16,8},{24,16},{0,24},{9,1},{17,9},{25,17},{1,25},{10,2},{18... | collective-permute-start | bytes 6152 | tf_op jit(solution)/shard_map/ppermute | solution.py:19
  4.0 6.9 %collective-permute-start = (f32[1,1,4,64]{3,2,1,0:T(4,128)S(1)}, f32[1,1,4,64]{3,2,1,0:T(4,128)S(1)}, u32[]{:S(2)}, u32[]{:S(2)}) collective-permute-start(f32[1,1,4,64]{3,2,1,0:T(4,128)S(1)} %get-tuple-element.79), channel_id=1, source_target_pairs={{0,1},{1,2},{2,3},{3,4},{4,5},{5,6},{6,7},{7,0},{8,9},{9,10},{10,1... | collective-permute-start | bytes 3080 | tf_op jit(solution)/shard_map/ppermute | solution.py:17
  6.2 3.1 copy-start.5
  6.2 4.6 collective-permute-start.1
  20.5 0.7 copy-start.3
  42.4 0.7 copy-start.4
  43.6 6.5 %collective-permute-start.6 = (f32[1,2,4,64]{3,2,1,0:T(4,128)S(1)}, f32[1,2,4,64]{3,2,1,0:T(4,128)S(1)}, u32[]{:S(2)}, u32[]{:S(2)}) collective-permute-start(f32[1,2,4,64]{3,2,1,0:T(4,128)S(1)} %get-tuple-element.73), channel_id=1, source_target_pairs={{0,8},{8,16},{16,24},{24,0},{1,9},{9,17},{17,25},{25,1},{2,10},{10... | collective-permute-start | bytes 6152 | tf_op jit(solution)/shard_map/ppermute | solution.py:17
  43.6 8.0 %collective-permute-start.7 = (f32[1,2,4,64]{3,2,1,0:T(4,128)S(1)}, f32[1,2,4,64]{3,2,1,0:T(4,128)S(1)}, u32[]{:S(2)}, u32[]{:S(2)}) collective-permute-start(f32[1,2,4,64]{3,2,1,0:T(4,128)S(1)} %get-tuple-element.73), channel_id=1, source_target_pairs={{8,0},{16,8},{24,16},{0,24},{9,1},{17,9},{25,17},{1,25},{10,2},{18... | collective-permute-start | bytes 6152 | tf_op jit(solution)/shard_map/ppermute | solution.py:19
  45.4 6.3 %collective-permute-start.4 = (f32[1,1,4,64]{3,2,1,0:T(4,128)S(1)}, f32[1,1,4,64]{3,2,1,0:T(4,128)S(1)}, u32[]{:S(2)}, u32[]{:S(2)}) collective-permute-start(f32[1,1,4,64]{3,2,1,0:T(4,128)S(1)} %get-tuple-element.75), channel_id=1, source_target_pairs={{0,1},{1,2},{2,3},{3,4},{4,5},{5,6},{6,7},{7,0},{8,9},{9,10},{10,1... | collective-permute-start | bytes 3080 | tf_op jit(solution)/shard_map/ppermute | solution.py:17
  45.4 6.3 %collective-permute-start.5 = (f32[1,1,4,64]{3,2,1,0:T(4,128)S(1)}, f32[1,1,4,64]{3,2,1,0:T(4,128)S(1)}, u32[]{:S(2)}, u32[]{:S(2)}) collective-permute-start(f32[1,1,4,64]{3,2,1,0:T(4,128)S(1)} %get-tuple-element.76), channel_id=1, source_target_pairs={{1,0},{2,1},{3,2},{4,3},{5,4},{6,5},{7,6},{0,7},{9,8},{10,9},{11,1... | collective-permute-start | bytes 3080 | tf_op jit(solution)/shard_map/ppermute | solution.py:19
  61.4 6.5 %collective-permute-start.10 = (f32[1,2,4,64]{3,2,1,0:T(4,128)S(1)}, f32[1,2,4,64]{3,2,1,0:T(4,128)S(1)}, u32[]{:S(2)}, u32[]{:S(2)}) collective-permute-start(f32[1,2,4,64]{3,2,1,0:T(4,128)S(1)} %get-tuple-element.69), channel_id=1, source_target_pairs={{0,8},{8,16},{16,24},{24,0},{1,9},{9,17},{17,25},{25,1},{2,10},{10... | collective-permute-start | bytes 6152 | tf_op jit(solution)/shard_map/ppermute | solution.py:17
  61.5 8.0 %collective-permute-start.11 = (f32[1,2,4,64]{3,2,1,0:T(4,128)S(1)}, f32[1,2,4,64]{3,2,1,0:T(4,128)S(1)}, u32[]{:S(2)}, u32[]{:S(2)}) collective-permute-start(f32[1,2,4,64]{3,2,1,0:T(4,128)S(1)} %get-tuple-element.69), channel_id=1, source_target_pairs={{8,0},{16,8},{24,16},{0,24},{9,1},{17,9},{25,17},{1,25},{10,2},{18... | collective-permute-start | bytes 6152 | tf_op jit(solution)/shard_map/ppermute | solution.py:19
  63.2 6.3 %collective-permute-start.8 = (f32[1,1,4,64]{3,2,1,0:T(4,128)S(1)}, f32[1,1,4,64]{3,2,1,0:T(4,128)S(1)}, u32[]{:S(2)}, u32[]{:S(2)}) collective-permute-start(f32[1,1,4,64]{3,2,1,0:T(4,128)S(1)} %get-tuple-element.71), channel_id=1, source_target_pairs={{0,1},{1,2},{2,3},{3,4},{4,5},{5,6},{6,7},{7,0},{8,9},{9,10},{10,1... | collective-permute-start | bytes 3080 | tf_op jit(solution)/shard_map/ppermute | solution.py:17
  63.2 6.3 %collective-permute-start.9 = (f32[1,1,4,64]{3,2,1,0:T(4,128)S(1)}, f32[1,1,4,64]{3,2,1,0:T(4,128)S(1)}, u32[]{:S(2)}, u32[]{:S(2)}) collective-permute-start(f32[1,1,4,64]{3,2,1,0:T(4,128)S(1)} %get-tuple-element.72), channel_id=1, source_target_pairs={{1,0},{2,1},{3,2},{4,3},{5,4},{6,5},{7,6},{0,7},{9,8},{10,9},{11,1... | collective-permute-start | bytes 3080 | tf_op jit(solution)/shard_map/ppermute | solution.py:19
  69.6 9.6 %copy-start.1 = (f32[1,2,128,128]{3,2,1,0:T(8,128)S(1)}, f32[1,2,128,128]{3,2,1,0:T(8,128)}, u32[]{:S(2)}) copy-start(f32[1,2,128,128]{3,2,1,0:T(8,128)} %param.10) | copy-start | bytes 393220
  79.6 6.5 %collective-permute-start.14 = (f32[1,2,4,64]{3,2,1,0:T(4,128)S(1)}, f32[1,2,4,64]{3,2,1,0:T(4,128)S(1)}, u32[]{:S(2)}, u32[]{:S(2)}) collective-permute-start(f32[1,2,4,64]{3,2,1,0:T(4,128)S(1)} %get-tuple-element.65), channel_id=1, source_target_pairs={{0,8},{8,16},{16,24},{24,0},{1,9},{9,17},{17,25},{25,1},{2,10},{10... | collective-permute-start | bytes 6152 | tf_op jit(solution)/shard_map/ppermute | solution.py:17
  79.6 8.0 %collective-permute-start.15 = (f32[1,2,4,64]{3,2,1,0:T(4,128)S(1)}, f32[1,2,4,64]{3,2,1,0:T(4,128)S(1)}, u32[]{:S(2)}, u32[]{:S(2)}) collective-permute-start(f32[1,2,4,64]{3,2,1,0:T(4,128)S(1)} %get-tuple-element.65), channel_id=1, source_target_pairs={{8,0},{16,8},{24,16},{0,24},{9,1},{17,9},{25,17},{1,25},{10,2},{18... | collective-permute-start | bytes 6152 | tf_op jit(solution)/shard_map/ppermute | solution.py:19
  81.3 6.3 %collective-permute-start.12 = (f32[1,1,4,64]{3,2,1,0:T(4,128)S(1)}, f32[1,1,4,64]{3,2,1,0:T(4,128)S(1)}, u32[]{:S(2)}, u32[]{:S(2)}) collective-permute-start(f32[1,1,4,64]{3,2,1,0:T(4,128)S(1)} %get-tuple-element.67), channel_id=1, source_target_pairs={{0,1},{1,2},{2,3},{3,4},{4,5},{5,6},{6,7},{7,0},{8,9},{9,10},{10,1... | collective-permute-start | bytes 3080 | tf_op jit(solution)/shard_map/ppermute | solution.py:17
  81.3 6.3 %collective-permute-start.13 = (f32[1,1,4,64]{3,2,1,0:T(4,128)S(1)}, f32[1,1,4,64]{3,2,1,0:T(4,128)S(1)}, u32[]{:S(2)}, u32[]{:S(2)}) collective-permute-start(f32[1,1,4,64]{3,2,1,0:T(4,128)S(1)} %get-tuple-element.68), channel_id=1, source_target_pairs={{1,0},{2,1},{3,2},{4,3},{5,4},{6,5},{7,6},{0,7},{9,8},{10,9},{11,1... | collective-permute-start | bytes 3080 | tf_op jit(solution)/shard_map/ppermute | solution.py:19
  97.4 6.5 %collective-permute-start.18 = (f32[1,2,4,64]{3,2,1,0:T(4,128)S(1)}, f32[1,2,4,64]{3,2,1,0:T(4,128)S(1)}, u32[]{:S(2)}, u32[]{:S(2)}) collective-permute-start(f32[1,2,4,64]{3,2,1,0:T(4,128)S(1)} %get-tuple-element.61), channel_id=1, source_target_pairs={{0,8},{8,16},{16,24},{24,0},{1,9},{9,17},{17,25},{25,1},{2,10},{10... | collective-permute-start | bytes 6152 | tf_op jit(solution)/shard_map/ppermute | solution.py:17
  97.4 8.0 %collective-permute-start.19 = (f32[1,2,4,64]{3,2,1,0:T(4,128)S(1)}, f32[1,2,4,64]{3,2,1,0:T(4,128)S(1)}, u32[]{:S(2)}, u32[]{:S(2)}) collective-permute-start(f32[1,2,4,64]{3,2,1,0:T(4,128)S(1)} %get-tuple-element.61), channel_id=1, source_target_pairs={{8,0},{16,8},{24,16},{0,24},{9,1},{17,9},{25,17},{1,25},{10,2},{18... | collective-permute-start | bytes 6152 | tf_op jit(solution)/shard_map/ppermute | solution.py:19
  99.2 6.3 %collective-permute-start.16 = (f32[1,1,4,64]{3,2,1,0:T(4,128)S(1)}, f32[1,1,4,64]{3,2,1,0:T(4,128)S(1)}, u32[]{:S(2)}, u32[]{:S(2)}) collective-permute-start(f32[1,1,4,64]{3,2,1,0:T(4,128)S(1)} %get-tuple-element.63), channel_id=1, source_target_pairs={{0,1},{1,2},{2,3},{3,4},{4,5},{5,6},{6,7},{7,0},{8,9},{9,10},{10,1... | collective-permute-start | bytes 3080 | tf_op jit(solution)/shard_map/ppermute | solution.py:17
  99.2 6.3 %collective-permute-start.17 = (f32[1,1,4,64]{3,2,1,0:T(4,128)S(1)}, f32[1,1,4,64]{3,2,1,0:T(4,128)S(1)}, u32[]{:S(2)}, u32[]{:S(2)}) collective-permute-start(f32[1,1,4,64]{3,2,1,0:T(4,128)S(1)} %get-tuple-element.64), channel_id=1, source_target_pairs={{1,0},{2,1},{3,2},{4,3},{5,4},{6,5},{7,6},{0,7},{9,8},{10,9},{11,1... | collective-permute-start | bytes 3080 | tf_op jit(solution)/shard_map/ppermute | solution.py:19
  136.8 6.5 %collective-permute-start.22 = (f32[1,2,4,64]{3,2,1,0:T(4,128)S(1)}, f32[1,2,4,64]{3,2,1,0:T(4,128)S(1)}, u32[]{:S(2)}, u32[]{:S(2)}) collective-permute-start(f32[1,2,4,64]{3,2,1,0:T(4,128)S(1)} %get-tuple-element.57), channel_id=1, source_target_pairs={{0,8},{8,16},{16,24},{24,0},{1,9},{9,17},{17,25},{25,1},{2,10},{10... | collective-permute-start | bytes 6152 | tf_op jit(solution)/shard_map/ppermute | solution.py:17
  136.8 8.0 %collective-permute-start.23 = (f32[1,2,4,64]{3,2,1,0:T(4,128)S(1)}, f32[1,2,4,64]{3,2,1,0:T(4,128)S(1)}, u32[]{:S(2)}, u32[]{:S(2)}) collective-permute-start(f32[1,2,4,64]{3,2,1,0:T(4,128)S(1)} %get-tuple-element.57), channel_id=1, source_target_pairs={{8,0},{16,8},{24,16},{0,24},{9,1},{17,9},{25,17},{1,25},{10,2},{18... | collective-permute-start | bytes 6152 | tf_op jit(solution)/shard_map/ppermute | solution.py:19
  138.6 6.3 %collective-permute-start.20 = (f32[1,1,4,64]{3,2,1,0:T(4,128)S(1)}, f32[1,1,4,64]{3,2,1,0:T(4,128)S(1)}, u32[]{:S(2)}, u32[]{:S(2)}) collective-permute-start(f32[1,1,4,64]{3,2,1,0:T(4,128)S(1)} %get-tuple-element.59), channel_id=1, source_target_pairs={{0,1},{1,2},{2,3},{3,4},{4,5},{5,6},{6,7},{7,0},{8,9},{9,10},{10,1... | collective-permute-start | bytes 3080 | tf_op jit(solution)/shard_map/ppermute | solution.py:17
  138.6 6.3 %collective-permute-start.21 = (f32[1,1,4,64]{3,2,1,0:T(4,128)S(1)}, f32[1,1,4,64]{3,2,1,0:T(4,128)S(1)}, u32[]{:S(2)}, u32[]{:S(2)}) collective-permute-start(f32[1,1,4,64]{3,2,1,0:T(4,128)S(1)} %get-tuple-element.60), channel_id=1, source_target_pairs={{1,0},{2,1},{3,2},{4,3},{5,4},{6,5},{7,6},{0,7},{9,8},{10,9},{11,1... | collective-permute-start | bytes 3080 | tf_op jit(solution)/shard_map/ppermute | solution.py:19
  195.1 6.5 %collective-permute-start.26 = (f32[1,2,4,64]{3,2,1,0:T(4,128)S(1)}, f32[1,2,4,64]{3,2,1,0:T(4,128)S(1)}, u32[]{:S(2)}, u32[]{:S(2)}) collective-permute-start(f32[1,2,4,64]{3,2,1,0:T(4,128)S(1)} %get-tuple-element.53), channel_id=1, source_target_pairs={{0,8},{8,16},{16,24},{24,0},{1,9},{9,17},{17,25},{25,1},{2,10},{10... | collective-permute-start | bytes 6152 | tf_op jit(solution)/shard_map/ppermute | solution.py:17
  195.1 8.0 %collective-permute-start.27 = (f32[1,2,4,64]{3,2,1,0:T(4,128)S(1)}, f32[1,2,4,64]{3,2,1,0:T(4,128)S(1)}, u32[]{:S(2)}, u32[]{:S(2)}) collective-permute-start(f32[1,2,4,64]{3,2,1,0:T(4,128)S(1)} %get-tuple-element.53), channel_id=1, source_target_pairs={{8,0},{16,8},{24,16},{0,24},{9,1},{17,9},{25,17},{1,25},{10,2},{18... | collective-permute-start | bytes 6152 | tf_op jit(solution)/shard_map/ppermute | solution.py:19
  196.8 6.3 %collective-permute-start.24 = (f32[1,1,4,64]{3,2,1,0:T(4,128)S(1)}, f32[1,1,4,64]{3,2,1,0:T(4,128)S(1)}, u32[]{:S(2)}, u32[]{:S(2)}) collective-permute-start(f32[1,1,4,64]{3,2,1,0:T(4,128)S(1)} %get-tuple-element.55), channel_id=1, source_target_pairs={{0,1},{1,2},{2,3},{3,4},{4,5},{5,6},{6,7},{7,0},{8,9},{9,10},{10,1... | collective-permute-start | bytes 3080 | tf_op jit(solution)/shard_map/ppermute | solution.py:17
  199.1 4.0 collective-permute-start.25
  213.2 6.5 %collective-permute-start.30 = (f32[1,2,4,64]{3,2,1,0:T(4,128)S(1)}, f32[1,2,4,64]{3,2,1,0:T(4,128)S(1)}, u32[]{:S(2)}, u32[]{:S(2)}) collective-permute-start(f32[1,2,4,64]{3,2,1,0:T(4,128)S(1)} %get-tuple-element.49), channel_id=1, source_target_pairs={{0,8},{8,16},{16,24},{24,0},{1,9},{9,17},{17,25},{25,1},{2,10},{10... | collective-permute-start | bytes 6152 | tf_op jit(solution)/shard_map/ppermute | solution.py:17
  213.2 8.0 %collective-permute-start.31 = (f32[1,2,4,64]{3,2,1,0:T(4,128)S(1)}, f32[1,2,4,64]{3,2,1,0:T(4,128)S(1)}, u32[]{:S(2)}, u32[]{:S(2)}) collective-permute-start(f32[1,2,4,64]{3,2,1,0:T(4,128)S(1)} %get-tuple-element.49), channel_id=1, source_target_pairs={{8,0},{16,8},{24,16},{0,24},{9,1},{17,9},{25,17},{1,25},{10,2},{18... | collective-permute-start | bytes 6152 | tf_op jit(solution)/shard_map/ppermute | solution.py:19
  214.9 6.3 %collective-permute-start.28 = (f32[1,1,4,64]{3,2,1,0:T(4,128)S(1)}, f32[1,1,4,64]{3,2,1,0:T(4,128)S(1)}, u32[]{:S(2)}, u32[]{:S(2)}) collective-permute-start(f32[1,1,4,64]{3,2,1,0:T(4,128)S(1)} %get-tuple-element.51), channel_id=1, source_target_pairs={{0,1},{1,2},{2,3},{3,4},{4,5},{5,6},{6,7},{7,0},{8,9},{9,10},{10,1... | collective-permute-start | bytes 3080 | tf_op jit(solution)/shard_map/ppermute | solution.py:17
  216.7 4.5 collective-permute-start.29
  231.0 6.5 %collective-permute-start.34 = (f32[1,2,4,64]{3,2,1,0:T(4,128)S(1)}, f32[1,2,4,64]{3,2,1,0:T(4,128)S(1)}, u32[]{:S(2)}, u32[]{:S(2)}) collective-permute-start(f32[1,2,4,64]{3,2,1,0:T(4,128)S(1)} %get-tuple-element.45), channel_id=1, source_target_pairs={{0,8},{8,16},{16,24},{24,0},{1,9},{9,17},{17,25},{25,1},{2,10},{10... | collective-permute-start | bytes 6152 | tf_op jit(solution)/shard_map/ppermute | solution.py:17
  231.0 8.0 %collective-permute-start.35 = (f32[1,2,4,64]{3,2,1,0:T(4,128)S(1)}, f32[1,2,4,64]{3,2,1,0:T(4,128)S(1)}, u32[]{:S(2)}, u32[]{:S(2)}) collective-permute-start(f32[1,2,4,64]{3,2,1,0:T(4,128)S(1)} %get-tuple-element.45), channel_id=1, source_target_pairs={{8,0},{16,8},{24,16},{0,24},{9,1},{17,9},{25,17},{1,25},{10,2},{18... | collective-permute-start | bytes 6152 | tf_op jit(solution)/shard_map/ppermute | solution.py:19
  232.8 6.3 %collective-permute-start.32 = (f32[1,1,4,64]{3,2,1,0:T(4,128)S(1)}, f32[1,1,4,64]{3,2,1,0:T(4,128)S(1)}, u32[]{:S(2)}, u32[]{:S(2)}) collective-permute-start(f32[1,1,4,64]{3,2,1,0:T(4,128)S(1)} %get-tuple-element.47), channel_id=1, source_target_pairs={{0,1},{1,2},{2,3},{3,4},{4,5},{5,6},{6,7},{7,0},{8,9},{9,10},{10,1... | collective-permute-start | bytes 3080 | tf_op jit(solution)/shard_map/ppermute | solution.py:17
  234.1 4.9 %collective-permute-start.33 = (f32[1,1,4,64]{3,2,1,0:T(4,128)S(1)}, f32[1,1,4,64]{3,2,1,0:T(4,128)S(1)}, u32[]{:S(2)}, u32[]{:S(2)}) collective-permute-start(f32[1,1,4,64]{3,2,1,0:T(4,128)S(1)} %get-tuple-element.48), channel_id=1, source_target_pairs={{1,0},{2,1},{3,2},{4,3},{5,4},{6,5},{7,6},{0,7},{9,8},{10,9},{11,1... | collective-permute-start | bytes 3080 | tf_op jit(solution)/shard_map/ppermute | solution.py:19
  270.4 6.5 %collective-permute-start.38 = (f32[1,2,4,64]{3,2,1,0:T(4,128)S(1)}, f32[1,2,4,64]{3,2,1,0:T(4,128)S(1)}, u32[]{:S(2)}, u32[]{:S(2)}) collective-permute-start(f32[1,2,4,64]{3,2,1,0:T(4,128)S(1)} %get-tuple-element.41), channel_id=1, source_target_pairs={{0,8},{8,16},{16,24},{24,0},{1,9},{9,17},{17,25},{25,1},{2,10},{10... | collective-permute-start | bytes 6152 | tf_op jit(solution)/shard_map/ppermute | solution.py:17
  270.4 8.0 %collective-permute-start.39 = (f32[1,2,4,64]{3,2,1,0:T(4,128)S(1)}, f32[1,2,4,64]{3,2,1,0:T(4,128)S(1)}, u32[]{:S(2)}, u32[]{:S(2)}) collective-permute-start(f32[1,2,4,64]{3,2,1,0:T(4,128)S(1)} %get-tuple-element.41), channel_id=1, source_target_pairs={{8,0},{16,8},{24,16},{0,24},{9,1},{17,9},{25,17},{1,25},{10,2},{18... | collective-permute-start | bytes 6152 | tf_op jit(solution)/shard_map/ppermute | solution.py:19
  272.2 6.3 %collective-permute-start.36 = (f32[1,1,4,64]{3,2,1,0:T(4,128)S(1)}, f32[1,1,4,64]{3,2,1,0:T(4,128)S(1)}, u32[]{:S(2)}, u32[]{:S(2)}) collective-permute-start(f32[1,1,4,64]{3,2,1,0:T(4,128)S(1)} %get-tuple-element.43), channel_id=1, source_target_pairs={{0,1},{1,2},{2,3},{3,4},{4,5},{5,6},{6,7},{7,0},{8,9},{9,10},{10,1... | collective-permute-start | bytes 3080 | tf_op jit(solution)/shard_map/ppermute | solution.py:17
  272.2 6.3 %collective-permute-start.37 = (f32[1,1,4,64]{3,2,1,0:T(4,128)S(1)}, f32[1,1,4,64]{3,2,1,0:T(4,128)S(1)}, u32[]{:S(2)}, u32[]{:S(2)}) collective-permute-start(f32[1,1,4,64]{3,2,1,0:T(4,128)S(1)} %get-tuple-element.44), channel_id=1, source_target_pairs={{1,0},{2,1},{3,2},{4,3},{5,4},{6,5},{7,6},{0,7},{9,8},{10,9},{11,1... | collective-permute-start | bytes 3080 | tf_op jit(solution)/shard_map/ppermute | solution.py:19
  329.3 6.5 %collective-permute-start.42 = (f32[1,2,4,64]{3,2,1,0:T(4,128)S(1)}, f32[1,2,4,64]{3,2,1,0:T(4,128)S(1)}, u32[]{:S(2)}, u32[]{:S(2)}) collective-permute-start(f32[1,2,4,64]{3,2,1,0:T(4,128)S(1)} %get-tuple-element.37), channel_id=1, source_target_pairs={{0,8},{8,16},{16,24},{24,0},{1,9},{9,17},{17,25},{25,1},{2,10},{10... | collective-permute-start | bytes 6152 | tf_op jit(solution)/shard_map/ppermute | solution.py:17
  329.3 8.0 %collective-permute-start.43 = (f32[1,2,4,64]{3,2,1,0:T(4,128)S(1)}, f32[1,2,4,64]{3,2,1,0:T(4,128)S(1)}, u32[]{:S(2)}, u32[]{:S(2)}) collective-permute-start(f32[1,2,4,64]{3,2,1,0:T(4,128)S(1)} %get-tuple-element.37), channel_id=1, source_target_pairs={{8,0},{16,8},{24,16},{0,24},{9,1},{17,9},{25,17},{1,25},{10,2},{18... | collective-permute-start | bytes 6152 | tf_op jit(solution)/shard_map/ppermute | solution.py:19
  331.1 6.3 %collective-permute-start.40 = (f32[1,1,4,64]{3,2,1,0:T(4,128)S(1)}, f32[1,1,4,64]{3,2,1,0:T(4,128)S(1)}, u32[]{:S(2)}, u32[]{:S(2)}) collective-permute-start(f32[1,1,4,64]{3,2,1,0:T(4,128)S(1)} %get-tuple-element.39), channel_id=1, source_target_pairs={{0,1},{1,2},{2,3},{3,4},{4,5},{5,6},{6,7},{7,0},{8,9},{9,10},{10,1... | collective-permute-start | bytes 3080 | tf_op jit(solution)/shard_map/ppermute | solution.py:17
  333.3 4.0 collective-permute-start.41
  347.4 6.5 %collective-permute-start.46 = (f32[1,2,4,64]{3,2,1,0:T(4,128)S(1)}, f32[1,2,4,64]{3,2,1,0:T(4,128)S(1)}, u32[]{:S(2)}, u32[]{:S(2)}) collective-permute-start(f32[1,2,4,64]{3,2,1,0:T(4,128)S(1)} %get-tuple-element.33), channel_id=1, source_target_pairs={{0,8},{8,16},{16,24},{24,0},{1,9},{9,17},{17,25},{25,1},{2,10},{10... | collective-permute-start | bytes 6152 | tf_op jit(solution)/shard_map/ppermute | solution.py:17
  347.4 8.0 %collective-permute-start.47 = (f32[1,2,4,64]{3,2,1,0:T(4,128)S(1)}, f32[1,2,4,64]{3,2,1,0:T(4,128)S(1)}, u32[]{:S(2)}, u32[]{:S(2)}) collective-permute-start(f32[1,2,4,64]{3,2,1,0:T(4,128)S(1)} %get-tuple-element.33), channel_id=1, source_target_pairs={{8,0},{16,8},{24,16},{0,24},{9,1},{17,9},{25,17},{1,25},{10,2},{18... | collective-permute-start | bytes 6152 | tf_op jit(solution)/shard_map/ppermute | solution.py:19
  349.2 6.3 %collective-permute-start.44 = (f32[1,1,4,64]{3,2,1,0:T(4,128)S(1)}, f32[1,1,4,64]{3,2,1,0:T(4,128)S(1)}, u32[]{:S(2)}, u32[]{:S(2)}) collective-permute-start(f32[1,1,4,64]{3,2,1,0:T(4,128)S(1)} %get-tuple-element.35), channel_id=1, source_target_pairs={{0,1},{1,2},{2,3},{3,4},{4,5},{5,6},{6,7},{7,0},{8,9},{9,10},{10,1... | collective-permute-start | bytes 3080 | tf_op jit(solution)/shard_map/ppermute | solution.py:17
  351.0 4.5 collective-permute-start.45
  365.2 6.5 %collective-permute-start.50 = (f32[1,2,4,64]{3,2,1,0:T(4,128)S(1)}, f32[1,2,4,64]{3,2,1,0:T(4,128)S(1)}, u32[]{:S(2)}, u32[]{:S(2)}) collective-permute-start(f32[1,2,4,64]{3,2,1,0:T(4,128)S(1)} %get-tuple-element.29), channel_id=1, source_target_pairs={{0,8},{8,16},{16,24},{24,0},{1,9},{9,17},{17,25},{25,1},{2,10},{10... | collective-permute-start | bytes 6152 | tf_op jit(solution)/shard_map/ppermute | solution.py:17
  365.3 8.0 %collective-permute-start.51 = (f32[1,2,4,64]{3,2,1,0:T(4,128)S(1)}, f32[1,2,4,64]{3,2,1,0:T(4,128)S(1)}, u32[]{:S(2)}, u32[]{:S(2)}) collective-permute-start(f32[1,2,4,64]{3,2,1,0:T(4,128)S(1)} %get-tuple-element.29), channel_id=1, source_target_pairs={{8,0},{16,8},{24,16},{0,24},{9,1},{17,9},{25,17},{1,25},{10,2},{18... | collective-permute-start | bytes 6152 | tf_op jit(solution)/shard_map/ppermute | solution.py:19
  367.0 6.3 %collective-permute-start.48 = (f32[1,1,4,64]{3,2,1,0:T(4,128)S(1)}, f32[1,1,4,64]{3,2,1,0:T(4,128)S(1)}, u32[]{:S(2)}, u32[]{:S(2)}) collective-permute-start(f32[1,1,4,64]{3,2,1,0:T(4,128)S(1)} %get-tuple-element.31), channel_id=1, source_target_pairs={{0,1},{1,2},{2,3},{3,4},{4,5},{5,6},{6,7},{7,0},{8,9},{9,10},{10,1... | collective-permute-start | bytes 3080 | tf_op jit(solution)/shard_map/ppermute | solution.py:17
  368.4 4.9 %collective-permute-start.49 = (f32[1,1,4,64]{3,2,1,0:T(4,128)S(1)}, f32[1,1,4,64]{3,2,1,0:T(4,128)S(1)}, u32[]{:S(2)}, u32[]{:S(2)}) collective-permute-start(f32[1,1,4,64]{3,2,1,0:T(4,128)S(1)} %get-tuple-element.32), channel_id=1, source_target_pairs={{1,0},{2,1},{3,2},{4,3},{5,4},{6,5},{7,6},{0,7},{9,8},{10,9},{11,1... | collective-permute-start | bytes 3080 | tf_op jit(solution)/shard_map/ppermute | solution.py:19
  404.6 6.5 %collective-permute-start.54 = (f32[1,2,4,64]{3,2,1,0:T(4,128)S(1)}, f32[1,2,4,64]{3,2,1,0:T(4,128)S(1)}, u32[]{:S(2)}, u32[]{:S(2)}) collective-permute-start(f32[1,2,4,64]{3,2,1,0:T(4,128)S(1)} %get-tuple-element.25), channel_id=1, source_target_pairs={{0,8},{8,16},{16,24},{24,0},{1,9},{9,17},{17,25},{25,1},{2,10},{10... | collective-permute-start | bytes 6152 | tf_op jit(solution)/shard_map/ppermute | solution.py:17
  404.7 8.0 %collective-permute-start.55 = (f32[1,2,4,64]{3,2,1,0:T(4,128)S(1)}, f32[1,2,4,64]{3,2,1,0:T(4,128)S(1)}, u32[]{:S(2)}, u32[]{:S(2)}) collective-permute-start(f32[1,2,4,64]{3,2,1,0:T(4,128)S(1)} %get-tuple-element.25), channel_id=1, source_target_pairs={{8,0},{16,8},{24,16},{0,24},{9,1},{17,9},{25,17},{1,25},{10,2},{18... | collective-permute-start | bytes 6152 | tf_op jit(solution)/shard_map/ppermute | solution.py:19
  406.4 6.3 %collective-permute-start.52 = (f32[1,1,4,64]{3,2,1,0:T(4,128)S(1)}, f32[1,1,4,64]{3,2,1,0:T(4,128)S(1)}, u32[]{:S(2)}, u32[]{:S(2)}) collective-permute-start(f32[1,1,4,64]{3,2,1,0:T(4,128)S(1)} %get-tuple-element.27), channel_id=1, source_target_pairs={{0,1},{1,2},{2,3},{3,4},{4,5},{5,6},{6,7},{7,0},{8,9},{9,10},{10,1... | collective-permute-start | bytes 3080 | tf_op jit(solution)/shard_map/ppermute | solution.py:17
  406.4 6.3 %collective-permute-start.53 = (f32[1,1,4,64]{3,2,1,0:T(4,128)S(1)}, f32[1,1,4,64]{3,2,1,0:T(4,128)S(1)}, u32[]{:S(2)}, u32[]{:S(2)}) collective-permute-start(f32[1,1,4,64]{3,2,1,0:T(4,128)S(1)} %get-tuple-element.28), channel_id=1, source_target_pairs={{1,0},{2,1},{3,2},{4,3},{5,4},{6,5},{7,6},{0,7},{9,8},{10,9},{11,1... | collective-permute-start | bytes 3080 | tf_op jit(solution)/shard_map/ppermute | solution.py:19
where the time goes:
time: 465 us; the launch traced here: 464 us
  blocking collectives  206 us (44%)
  local copies, waits for them, and re-layouts  139 us (30%)
  starting transfers between devices  92 us (20%)
  waiting for transfers between devices  20.7 us (4%)
    gather x14, local copies, waits for them, and re-layouts, jump(): picked = jnp.take_along_axis(facing, position, axis=-1)  134 us
    psum x3, blocking collectives, global_sums(): return lax.psum((first_dot, second_dot), ('srow', 'scol'))  122 us
    all_gather x4, blocking collectives, apply_inverse(): lax.all_gather(coarse_in, 'scol', axis=0, tiled=True)  84.1 us
    ppermute x28, starting transfers between devices, with_halo(): lax.ppermute(head, axis, [((i + 1) % count, i) for i in range(count)])  78.3 us
    ppermute x28, waiting for transfers between devices, with_halo(): lax.ppermute(tail, axis, [(i, (i + 1) % count) for i in range(count)])  20.7 us
    ppermute x28, starting transfers between devices, with_halo(): lax.ppermute(tail, axis, [(i, (i + 1) % count) for i in range(count)])  13.7 us
  transfers between devices with their start and end apart: 56, of which 14 were waited for; matrix products, arithmetic and copies ran while one was open for 0% of the time, Pallas kernels for 0%

commit v1 on v0

--- a/solution.py
+++ b/solution.py
@@ -5,6 +5,24 @@
 
 ITERS = 3
 precise = lax.Precision.HIGHEST
+
+
+def collect(value, axis, dim):
+    ways, here, step = (lax.axis_size(axis), lax.axis_index(axis), value.shape[dim])
+    dims = [n * ways if d == dim else n for d, n in enumerate(value.shape)]
+    full = lax.dynamic_update_slice_in_dim(
+        jnp.zeros(dims, value.dtype), value, here * step, axis=dim
+    )
+    going_up = going_down = value
+    for far in range(1, ways // 2 + 1):
+        going_up = lax.ppermute(going_up, axis, [(d, (d + 1) % ways) for d in range(ways)])
+        full = lax.dynamic_update_slice_in_dim(full, going_up, (here - far) % ways * step, axis=dim)
+        if 2 * far < ways:
+            going_down = lax.ppermute(going_down, axis, [(d, (d - 1) % ways) for d in range(ways)])
+            full = lax.dynamic_update_slice_in_dim(
+                full, going_down, (here + far) % ways * step, axis=dim
+            )
+    return full
 
 
 def with_halo(cells, sides, width):
@@ -52,7 +70,7 @@
     band_rows = coarse_inverse[0]
     coarse_out = jnp.dot(
         band_rows,
-        lax.all_gather(coarse_in, "scol", axis=0, tiled=True),
+        collect(coarse_in, "scol", 0),
         precision=precise,
         preferred_element_type=jnp.float32,
     )

time: 465 us -> 480 us (1.032)
  blocking collectives: 206 us -> 122 us
  starting transfers between devices: 92 us -> 149 us
  waiting for transfers between devices: 20.7 us -> 63.4 us
    all_gather x4 -> x0, blocking collectives: 84.1 us -> none  [apply_inverse(): lax.all_gather(coarse_in, 'scol', axis=0, tiled=True)]
    ppermute x0 -> x28, starting transfers between devices: none -> 56.8 us  [the longest x12 55 us: collect(): lax.ppermute(going_down, axis, [(d, (d - 1) % ways) for d in range(ways)])]
    ppermute x0 -> x28, waiting for transfers between devices: none -> 43.4 us  [the longest x16 43.3 us: collect(): lax.ppermute(going_up, axis, [(d, (d + 1) % ways) for d in range(ways)])]
  transfers between devices with their start and end apart: 56 -> 84, of which waited for: 14 -> 30; matrix products, arithmetic and copies ran while one was open for 0% -> 0% of each run, Pallas kernels for 0% -> 0%
where the time goes in v1:
time: 480 us
  starting transfers between devices  149 us (31%)
  local copies, waits for them, and re-layouts  139 us (29%)
  blocking collectives  122 us (25%)
  waiting for transfers between devices  63.4 us (13%)
    gather x14, local copies, waits for them, and re-layouts, jump(): picked = jnp.take_along_axis(facing, position, axis=-1)  134 us
    psum x3, blocking collectives, global_sums(): return lax.psum((first_dot, second_dot), ('srow', 'scol'))  122 us
    ppermute x28, starting transfers between devices, with_halo(): lax.ppermute(head, axis, [((i + 1) % count, i) for i in range(count)])  78.3 us
    ppermute x12, starting transfers between devices, collect(): lax.ppermute(going_down, axis, [(d, (d - 1) % ways) for d in range(ways)])  55 us
    ppermute x16, waiting for transfers between devices, collect(): lax.ppermute(going_up, axis, [(d, (d + 1) % ways) for d in range(ways)])  43.3 us
    ppermute x28, waiting for transfers between devices, with_halo(): lax.ppermute(tail, axis, [(i, (i + 1) % count) for i in range(count)])  19.9 us
    ppermute x28, starting transfers between devices, with_halo(): lax.ppermute(tail, axis, [(i, (i + 1) % count) for i in range(count)])  13.7 us
  transfers between devices with their start and end apart: 84, of which 30 were waited for; matrix products, arithmetic and copies ran while one was open for 0% of the time, Pallas kernels for 0%

profile of v1, /device:TPU:0, one launch (start us, length us, event | category | flops | bytes accessed | tf_op | source)
XLA Modules:
  0.0 479.8 jit_solution(257551321463149300)
XLA Ops:
  2.0 1.9 collective-permute-start.3
  4.0 2.3 collective-permute-start
  6.2 3.1 collective-permute-start.1
  10.9 9.6 %gather_fusion = f32[1024]{0:T(1024)S(1)} fusion(f32[2,4,128]{2,1,0:T(4,128)S(1)} %fusion.69, s32[1024]{0:T(1024)S(1)} %bitcast.204), kind=kCustom, calls=%fused_computation.clone | custom fusion | bytes 20480 | tf_op jit(solution)/shard_map/jit(take_along_axis)/gather | solution.py:61
  22.8 3.3 collective-permute-start.5
  27.7 4.7 collective-permute-start.7
  34.0 4.7 collective-permute-start.9
  40.3 6.2 %collective-permute-done.10 = f32[2,4]{1,0:T(2,128)S(1)} collective-permute-done((f32[2,4]{1,0:T(2,128)S(1)}, f32[2,4]{1,0:T(2,128)S(1)}, u32[]{:S(2)}, u32[]{:S(2)}) %collective-permute-start.10) | collective-permute-done | bytes 64 | tf_op jit(solution)/shard_map/ppermute | solution.py:18
  47.0 1.7 collective-permute-start.14
  48.8 4.7 collective-permute-start.12
  55.2 9.6 %gather_fusion.1 = f32[1024]{0:T(1024)S(1)} fusion(f32[2,4,128]{2,1,0:T(4,128)S(1)} %fusion.65, s32[1024]{0:T(1024)S(1)} %bitcast.205), kind=kCustom, calls=%fused_computation.1.clone | custom fusion | bytes 20480 | tf_op jit(solution)/shard_map/jit(take_along_axis)/gather | solution.py:61
  64.9 1.7 collective-permute-start.18
  66.6 4.7 collective-permute-start.16
  73.0 9.6 %gather_fusion.2 = f32[1024]{0:T(1024)S(1)} fusion(f32[2,4,128]{2,1,0:T(4,128)S(1)} %fusion.61, s32[1024]{0:T(1024)S(1)} %bitcast.206), kind=kCustom, calls=%fused_computation.2.clone | custom fusion | bytes 20480 | tf_op jit(solution)/shard_map/jit(take_along_axis)/gather | solution.py:61
  83.0 1.8 collective-permute-start.22
  84.8 4.7 collective-permute-start.20
  91.1 9.6 %gather_fusion.3 = f32[1024]{0:T(1024)S(1)} fusion(f32[2,4,128]{2,1,0:T(4,128)S(1)} %fusion.57, s32[1024]{0:T(1024)S(1)} %bitcast.207), kind=kCustom, calls=%fused_computation.3.clone | custom fusion | bytes 20480 | tf_op jit(solution)/shard_map/jit(take_along_axis)/gather | solution.py:61
  100.8 1.7 collective-permute-start.26
  102.6 4.7 collective-permute-start.24
  108.9 9.6 %gather_fusion.4 = f32[1024]{0:T(1024)S(1)} fusion(f32[2,4,128]{2,1,0:T(4,128)S(1)} %fusion.53, s32[1024]{0:T(1024)S(1)} %bitcast.208), kind=kCustom, calls=%fused_computation.4.clone | custom fusion | bytes 20480 | tf_op jit(solution)/shard_map/jit(take_along_axis)/gather | solution.py:61
  118.7 4.7 collective-permute-start.28
  125.0 4.7 collective-permute-start.30
  131.3 4.7 collective-permute-start.32
  137.6 6.2 %collective-permute-done.33 = f32[2,4]{1,0:T(2,128)S(1)} collective-permute-done((f32[2,4]{1,0:T(2,128)S(1)}, f32[2,4]{1,0:T(2,128)S(1)}, u32[]{:S(2)}, u32[]{:S(2)}) %collective-permute-start.33) | collective-permute-done | bytes 64 | tf_op jit(solution)/shard_map/ppermute | solution.py:18
  144.3 1.7 collective-permute-start.37
  146.1 4.7 collective-permute-start.35
  152.5 9.6 %gather_fusion.5 = f32[1024]{0:T(1024)S(1)} fusion(f32[2,4,128]{2,1,0:T(4,128)S(1)} %fusion.49, s32[1024]{0:T(1024)S(1)} %bitcast.209), kind=kCustom, calls=%fused_computation.5.clone | custom fusion | bytes 20480 | tf_op jit(solution)/shard_map/jit(take_along_axis)/gather | solution.py:61
  162.2 40.2 %all-reduce.2 = (f32[4]{0:T(128)S(1)}, f32[4]{0:T(128)S(1)}) all-reduce(f32[4]{0:T(128)S(1)} %get-tuple-element.8, f32[4]{0:T(128)S(1)} %get-tuple-element.7), channel_id=1, replica_groups=mesh['srow'=4,'scol'=8] {'srow','scol'}, use_global_device_ids=true, to_apply=%region_1.3 | all-reduce | flops 8 | bytes 64 | tf_op jit(solution)/shard_map/psum | solution.py:86
  202.6 1.7 collective-permute-start.41
  204.4 2.3 collective-permute-start.38
  206.6 2.4 collective-permute-start.39
  210.7 9.6 %gather_fusion.6 = f32[1024]{0:T(1024)S(1)} fusion(f32[2,4,128]{2,1,0:T(4,128)S(1)} %fusion.45, s32[1024]{0:T(1024)S(1)} %bitcast.210), kind=kCustom, calls=%fused_computation.6.clone | custom fusion | bytes 20480 | tf_op jit(solution)/shard_map/jit(take_along_axis)/gather | solution.py:61
  220.7 1.8 collective-permute-start.45
  222.5 1.8 collective-permute-start.42
  224.3 2.9 collective-permute-start.43
  228.8 9.6 %gather_fusion.7 = f32[1024]{0:T(1024)S(1)} fusion(f32[2,4,128]{2,1,0:T(4,128)S(1)} %fusion.41, s32[1024]{0:T(1024)S(1)} %bitcast.211), kind=kCustom, calls=%fused_computation.7.clone | custom fusion | bytes 20480 | tf_op jit(solution)/shard_map/jit(take_along_axis)/gather | solution.py:61
  241.7 3.4 collective-permute-start.47
  246.7 9.6 %gather_fusion.8 = f32[1024]{0:T(1024)S(1)} fusion(f32[2,4,128]{2,1,0:T(4,128)S(1)} %fusion.37, s32[1024]{0:T(1024)S(1)} %bitcast.212), kind=kCustom, calls=%fused_computation.8.clone | custom fusion | bytes 20480 | tf_op jit(solution)/shard_map/jit(take_along_axis)/gather | solution.py:61
  256.6 4.6 collective-permute-start.51
  262.7 4.7 collective-permute-start.53
  269.0 4.7 collective-permute-start.55
  275.3 6.2 %collective-permute-done.56 = f32[2,4]{1,0:T(2,128)S(1)} collective-permute-done((f32[2,4]{1,0:T(2,128)S(1)}, f32[2,4]{1,0:T(2,128)S(1)}, u32[]{:S(2)}, u32[]{:S(2)}) %collective-permute-start.56) | collective-permute-done | bytes 64 | tf_op jit(solution)/shard_map/ppermute | solution.py:18
  282.1 1.7 collective-permute-start.60
  283.8 4.7 collective-permute-start.58
  290.2 9.6 %gather_fusion.9 = f32[1024]{0:T(1024)S(1)} fusion(f32[2,4,128]{2,1,0:T(4,128)S(1)} %fusion.33, s32[1024]{0:T(1024)S(1)} %bitcast.213), kind=kCustom, calls=%fused_computation.9.clone | custom fusion | bytes 20480 | tf_op jit(solution)/shard_map/jit(take_along_axis)/gather | solution.py:61
  299.9 40.8 %all-reduce.1 = (f32[4]{0:T(128)S(1)}, f32[4]{0:T(128)S(1)}) all-reduce(f32[4]{0:T(128)S(1)} %get-tuple-element.6, f32[4]{0:T(128)S(1)} %get-tuple-element.5), channel_id=1, replica_groups=mesh['srow'=4,'scol'=8] {'srow','scol'}, use_global_device_ids=true, to_apply=%region_5.7 | all-reduce | flops 8 | bytes 64 | tf_op jit(solution)/shard_map/psum | solution.py:86
  340.9 1.8 collective-permute-start.64
  342.7 2.3 collective-permute-start.61
  345.0 2.4 collective-permute-start.62
  349.1 9.6 %gather_fusion.10 = f32[1024]{0:T(1024)S(1)} fusion(f32[2,4,128]{2,1,0:T(4,128)S(1)} %fusion.29, s32[1024]{0:T(1024)S(1)} %bitcast.214), kind=kCustom, calls=%fused_computation.10.clone | custom fusion | bytes 20480 | tf_op jit(solution)/shard_map/jit(take_along_axis)/gather | solution.py:61
  359.1 1.8 collective-permute-start.68
  360.8 1.8 collective-permute-start.65
  362.6 2.9 collective-permute-start.66
  367.2 9.6 %gather_fusion.11 = f32[1024]{0:T(1024)S(1)} fusion(f32[2,4,128]{2,1,0:T(4,128)S(1)} %fusion.25, s32[1024]{0:T(1024)S(1)} %bitcast.215), kind=kCustom, calls=%fused_computation.11.clone | custom fusion | bytes 20480 | tf_op jit(solution)/shard_map/jit(take_along_axis)/gather | solution.py:61
  380.0 3.4 collective-permute-start.70
  385.0 9.6 %gather_fusion.12 = f32[1024]{0:T(1024)S(1)} fusion(f32[2,4,128]{2,1,0:T(4,128)S(1)} %fusion.21, s32[1024]{0:T(1024)S(1)} %bitcast.216), kind=kCustom, calls=%fused_computation.12.clone | custom fusion | bytes 20480 | tf_op jit(solution)/shard_map/jit(take_along_axis)/gather | solution.py:61
  394.9 4.6 collective-permute-start.74
  401.1 4.7 collective-permute-start.76
  407.3 4.7 collective-permute-start.78
  413.6 6.2 %collective-permute-done.79 = f32[2,4]{1,0:T(2,128)S(1)} collective-permute-done((f32[2,4]{1,0:T(2,128)S(1)}, f32[2,4]{1,0:T(2,128)S(1)}, u32[]{:S(2)}, u32[]{:S(2)}) %collective-permute-start.79) | collective-permute-done | bytes 64 | tf_op jit(solution)/shard_map/ppermute | solution.py:18
  420.4 1.7 collective-permute-start.83
  422.2 4.7 collective-permute-start.81
  428.5 9.6 %gather_fusion.13 = f32[1024]{0:T(1024)S(1)} fusion(f32[2,4,128]{2,1,0:T(4,128)S(1)} %fusion.17, s32[1024]{0:T(1024)S(1)} %bitcast.217), kind=kCustom, calls=%fused_computation.13.clone | custom fusion | bytes 20480 | tf_op jit(solution)/shard_map/jit(take_along_axis)/gather | solution.py:61
  438.3 40.8 %all-reduce = (f32[4]{0:T(128)S(1)}, f32[4]{0:T(128)S(1)}) all-reduce(f32[4]{0:T(128)S(1)} %get-tuple-element.4, f32[4]{0:T(128)S(1)} %get-tuple-element.3), channel_id=1, replica_groups=mesh['srow'=4,'scol'=8] {'srow','scol'}, use_global_device_ids=true, to_apply=%region_9.11 | all-reduce | flops 8 | bytes 64 | tf_op jit(solution)/shard_map/psum | solution.py:86
  (259 shorter events, 57.1 us)
Async XLA Ops:
  1.5 8.6 %collective-permute-start.2 = (f32[1,2,4,64]{3,2,1,0:T(4,128)S(1)}, f32[1,2,4,64]{3,2,1,0:T(4,128)S(1)}, u32[]{:S(2)}, u32[]{:S(2)}) collective-permute-start(f32[1,2,4,64]{3,2,1,0:T(4,128)S(1)} %get-tuple-element.77), channel_id=1, source_target_pairs={{0,8},{8,16},{16,24},{24,0},{1,9},{9,17},{17,25},{25,1},{2,10},{10... | collective-permute-start | bytes 6152 | tf_op jit(solution)/shard_map/ppermute | solution.py:35
  2.0 8.8 %collective-permute-start.3 = (f32[1,2,4,64]{3,2,1,0:T(4,128)S(1)}, f32[1,2,4,64]{3,2,1,0:T(4,128)S(1)}, u32[]{:S(2)}, u32[]{:S(2)}) collective-permute-start(f32[1,2,4,64]{3,2,1,0:T(4,128)S(1)} %get-tuple-element.77), channel_id=1, source_target_pairs={{8,0},{16,8},{24,16},{0,24},{9,1},{17,9},{25,17},{1,25},{10,2},{18... | collective-permute-start | bytes 6152 | tf_op jit(solution)/shard_map/ppermute | solution.py:37
  4.0 6.9 %collective-permute-start = (f32[1,1,4,64]{3,2,1,0:T(4,128)S(1)}, f32[1,1,4,64]{3,2,1,0:T(4,128)S(1)}, u32[]{:S(2)}, u32[]{:S(2)}) collective-permute-start(f32[1,1,4,64]{3,2,1,0:T(4,128)S(1)} %get-tuple-element.79), channel_id=1, source_target_pairs={{0,1},{1,2},{2,3},{3,4},{4,5},{5,6},{6,7},{7,0},{8,9},{9,10},{10,1... | collective-permute-start | bytes 3080 | tf_op jit(solution)/shard_map/ppermute | solution.py:35
  21.3 6.3 %collective-permute-start.4 = (f32[2,4]{1,0:T(2,128)S(1)}, f32[2,4]{1,0:T(2,128)S(1)}, u32[]{:S(2)}, u32[]{:S(2)}) collective-permute-start(f32[2,4]{1,0:T(2,128)S(1)} %bitcast.269), channel_id=1, source_target_pairs={{0,1},{1,2},{2,3},{3,4},{4,5},{5,6},{6,7},{7,0},{8,9},{9,10},{10,1... | collective-permute-start | bytes 104 | tf_op jit(solution)/shard_map/ppermute | solution.py:18
  34.0 6.3 %collective-permute-start.9 = (f32[2,4]{1,0:T(2,128)S(1)}, f32[2,4]{1,0:T(2,128)S(1)}, u32[]{:S(2)}, u32[]{:S(2)}) collective-permute-start(f32[2,4]{1,0:T(2,128)S(1)} %collective-permute-done.7), channel_id=1, source_target_pairs={{0,7},{1,0},{2,1},{3,2},{4,3},{5,4},{6,5},{7,6},{8,15},{9,8},{10,9... | collective-permute-start | bytes 104 | tf_op jit(solution)/shard_map/ppermute | solution.py:21
  47.0 6.5 %collective-permute-start.13 = (f32[1,2,4,64]{3,2,1,0:T(4,128)S(1)}, f32[1,2,4,64]{3,2,1,0:T(4,128)S(1)}, u32[]{:S(2)}, u32[]{:S(2)}) collective-permute-start(f32[1,2,4,64]{3,2,1,0:T(4,128)S(1)} %get-tuple-element.73), channel_id=1, source_target_pairs={{0,8},{8,16},{16,24},{24,0},{1,9},{9,17},{17,25},{25,1},{2,10},{10... | collective-permute-start | bytes 6152 | tf_op jit(solution)/shard_map/ppermute | solution.py:35
  47.0 8.0 %collective-permute-start.14 = (f32[1,2,4,64]{3,2,1,0:T(4,128)S(1)}, f32[1,2,4,64]{3,2,1,0:T(4,128)S(1)}, u32[]{:S(2)}, u32[]{:S(2)}) collective-permute-start(f32[1,2,4,64]{3,2,1,0:T(4,128)S(1)} %get-tuple-element.73), channel_id=1, source_target_pairs={{8,0},{16,8},{24,16},{0,24},{9,1},{17,9},{25,17},{1,25},{10,2},{18... | collective-permute-start | bytes 6152 | tf_op jit(solution)/shard_map/ppermute | solution.py:37
  48.8 6.3 %collective-permute-start.11 = (f32[1,1,4,64]{3,2,1,0:T(4,128)S(1)}, f32[1,1,4,64]{3,2,1,0:T(4,128)S(1)}, u32[]{:S(2)}, u32[]{:S(2)}) collective-permute-start(f32[1,1,4,64]{3,2,1,0:T(4,128)S(1)} %get-tuple-element.75), channel_id=1, source_target_pairs={{0,1},{1,2},{2,3},{3,4},{4,5},{5,6},{6,7},{7,0},{8,9},{9,10},{10,1... | collective-permute-start | bytes 3080 | tf_op jit(solution)/shard_map/ppermute | solution.py:35
  48.8 6.3 %collective-permute-start.12 = (f32[1,1,4,64]{3,2,1,0:T(4,128)S(1)}, f32[1,1,4,64]{3,2,1,0:T(4,128)S(1)}, u32[]{:S(2)}, u32[]{:S(2)}) collective-permute-start(f32[1,1,4,64]{3,2,1,0:T(4,128)S(1)} %get-tuple-element.76), channel_id=1, source_target_pairs={{1,0},{2,1},{3,2},{4,3},{5,4},{6,5},{7,6},{0,7},{9,8},{10,9},{11,1... | collective-permute-start | bytes 3080 | tf_op jit(solution)/shard_map/ppermute | solution.py:37
  64.9 6.5 %collective-permute-start.17 = (f32[1,2,4,64]{3,2,1,0:T(4,128)S(1)}, f32[1,2,4,64]{3,2,1,0:T(4,128)S(1)}, u32[]{:S(2)}, u32[]{:S(2)}) collective-permute-start(f32[1,2,4,64]{3,2,1,0:T(4,128)S(1)} %get-tuple-element.69), channel_id=1, source_target_pairs={{0,8},{8,16},{16,24},{24,0},{1,9},{9,17},{17,25},{25,1},{2,10},{10... | collective-permute-start | bytes 6152 | tf_op jit(solution)/shard_map/ppermute | solution.py:35
  64.9 8.0 %collective-permute-start.18 = (f32[1,2,4,64]{3,2,1,0:T(4,128)S(1)}, f32[1,2,4,64]{3,2,1,0:T(4,128)S(1)}, u32[]{:S(2)}, u32[]{:S(2)}) collective-permute-start(f32[1,2,4,64]{3,2,1,0:T(4,128)S(1)} %get-tuple-element.69), channel_id=1, source_target_pairs={{8,0},{16,8},{24,16},{0,24},{9,1},{17,9},{25,17},{1,25},{10,2},{18... | collective-permute-start | bytes 6152 | tf_op jit(solution)/shard_map/ppermute | solution.py:37
  66.6 6.3 %collective-permute-start.15 = (f32[1,1,4,64]{3,2,1,0:T(4,128)S(1)}, f32[1,1,4,64]{3,2,1,0:T(4,128)S(1)}, u32[]{:S(2)}, u32[]{:S(2)}) collective-permute-start(f32[1,1,4,64]{3,2,1,0:T(4,128)S(1)} %get-tuple-element.71), channel_id=1, source_target_pairs={{0,1},{1,2},{2,3},{3,4},{4,5},{5,6},{6,7},{7,0},{8,9},{9,10},{10,1... | collective-permute-start | bytes 3080 | tf_op jit(solution)/shard_map/ppermute | solution.py:35
  66.6 6.3 %collective-permute-start.16 = (f32[1,1,4,64]{3,2,1,0:T(4,128)S(1)}, f32[1,1,4,64]{3,2,1,0:T(4,128)S(1)}, u32[]{:S(2)}, u32[]{:S(2)}) collective-permute-start(f32[1,1,4,64]{3,2,1,0:T(4,128)S(1)} %get-tuple-element.72), channel_id=1, source_target_pairs={{1,0},{2,1},{3,2},{4,3},{5,4},{6,5},{7,6},{0,7},{9,8},{10,9},{11,1... | collective-permute-start | bytes 3080 | tf_op jit(solution)/shard_map/ppermute | solution.py:37
  83.0 6.5 %collective-permute-start.21 = (f32[1,2,4,64]{3,2,1,0:T(4,128)S(1)}, f32[1,2,4,64]{3,2,1,0:T(4,128)S(1)}, u32[]{:S(2)}, u32[]{:S(2)}) collective-permute-start(f32[1,2,4,64]{3,2,1,0:T(4,128)S(1)} %get-tuple-element.65), channel_id=1, source_target_pairs={{0,8},{8,16},{16,24},{24,0},{1,9},{9,17},{17,25},{25,1},{2,10},{10... | collective-permute-start | bytes 6152 | tf_op jit(solution)/shard_map/ppermute | solution.py:35
  83.0 8.0 %collective-permute-start.22 = (f32[1,2,4,64]{3,2,1,0:T(4,128)S(1)}, f32[1,2,4,64]{3,2,1,0:T(4,128)S(1)}, u32[]{:S(2)}, u32[]{:S(2)}) collective-permute-start(f32[1,2,4,64]{3,2,1,0:T(4,128)S(1)} %get-tuple-element.65), channel_id=1, source_target_pairs={{8,0},{16,8},{24,16},{0,24},{9,1},{17,9},{25,17},{1,25},{10,2},{18... | collective-permute-start | bytes 6152 | tf_op jit(solution)/shard_map/ppermute | solution.py:37
  84.8 6.3 %collective-permute-start.19 = (f32[1,1,4,64]{3,2,1,0:T(4,128)S(1)}, f32[1,1,4,64]{3,2,1,0:T(4,128)S(1)}, u32[]{:S(2)}, u32[]{:S(2)}) collective-permute-start(f32[1,1,4,64]{3,2,1,0:T(4,128)S(1)} %get-tuple-element.67), channel_id=1, source_target_pairs={{0,1},{1,2},{2,3},{3,4},{4,5},{5,6},{6,7},{7,0},{8,9},{9,10},{10,1... | collective-permute-start | bytes 3080 | tf_op jit(solution)/shard_map/ppermute | solution.py:35
  84.8 6.3 %collective-permute-start.20 = (f32[1,1,4,64]{3,2,1,0:T(4,128)S(1)}, f32[1,1,4,64]{3,2,1,0:T(4,128)S(1)}, u32[]{:S(2)}, u32[]{:S(2)}) collective-permute-start(f32[1,1,4,64]{3,2,1,0:T(4,128)S(1)} %get-tuple-element.68), channel_id=1, source_target_pairs={{1,0},{2,1},{3,2},{4,3},{5,4},{6,5},{7,6},{0,7},{9,8},{10,9},{11,1... | collective-permute-start | bytes 3080 | tf_op jit(solution)/shard_map/ppermute | solution.py:37
  100.8 6.5 %collective-permute-start.25 = (f32[1,2,4,64]{3,2,1,0:T(4,128)S(1)}, f32[1,2,4,64]{3,2,1,0:T(4,128)S(1)}, u32[]{:S(2)}, u32[]{:S(2)}) collective-permute-start(f32[1,2,4,64]{3,2,1,0:T(4,128)S(1)} %get-tuple-element.61), channel_id=1, source_target_pairs={{0,8},{8,16},{16,24},{24,0},{1,9},{9,17},{17,25},{25,1},{2,10},{10... | collective-permute-start | bytes 6152 | tf_op jit(solution)/shard_map/ppermute | solution.py:35
  100.8 8.0 %collective-permute-start.26 = (f32[1,2,4,64]{3,2,1,0:T(4,128)S(1)}, f32[1,2,4,64]{3,2,1,0:T(4,128)S(1)}, u32[]{:S(2)}, u32[]{:S(2)}) collective-permute-start(f32[1,2,4,64]{3,2,1,0:T(4,128)S(1)} %get-tuple-element.61), channel_id=1, source_target_pairs={{8,0},{16,8},{24,16},{0,24},{9,1},{17,9},{25,17},{1,25},{10,2},{18... | collective-permute-start | bytes 6152 | tf_op jit(solution)/shard_map/ppermute | solution.py:37
  102.6 6.3 %collective-permute-start.23 = (f32[1,1,4,64]{3,2,1,0:T(4,128)S(1)}, f32[1,1,4,64]{3,2,1,0:T(4,128)S(1)}, u32[]{:S(2)}, u32[]{:S(2)}) collective-permute-start(f32[1,1,4,64]{3,2,1,0:T(4,128)S(1)} %get-tuple-element.63), channel_id=1, source_target_pairs={{0,1},{1,2},{2,3},{3,4},{4,5},{5,6},{6,7},{7,0},{8,9},{9,10},{10,1... | collective-permute-start | bytes 3080 | tf_op jit(solution)/shard_map/ppermute | solution.py:35
  102.6 6.3 %collective-permute-start.24 = (f32[1,1,4,64]{3,2,1,0:T(4,128)S(1)}, f32[1,1,4,64]{3,2,1,0:T(4,128)S(1)}, u32[]{:S(2)}, u32[]{:S(2)}) collective-permute-start(f32[1,1,4,64]{3,2,1,0:T(4,128)S(1)} %get-tuple-element.64), channel_id=1, source_target_pairs={{1,0},{2,1},{3,2},{4,3},{5,4},{6,5},{7,6},{0,7},{9,8},{10,9},{11,1... | collective-permute-start | bytes 3080 | tf_op jit(solution)/shard_map/ppermute | solution.py:37
  118.7 6.3 %collective-permute-start.27 = (f32[2,4]{1,0:T(2,128)S(1)}, f32[2,4]{1,0:T(2,128)S(1)}, u32[]{:S(2)}, u32[]{:S(2)}) collective-permute-start(f32[2,4]{1,0:T(2,128)S(1)} %bitcast.263), channel_id=1, source_target_pairs={{0,1},{1,2},{2,3},{3,4},{4,5},{5,6},{6,7},{7,0},{8,9},{9,10},{10,1... | collective-permute-start | bytes 104 | tf_op jit(solution)/shard_map/ppermute | solution.py:18
  118.7 6.3 %collective-permute-start.28 = (f32[2,4]{1,0:T(2,128)S(1)}, f32[2,4]{1,0:T(2,128)S(1)}, u32[]{:S(2)}, u32[]{:S(2)}) collective-permute-start(f32[2,4]{1,0:T(2,128)S(1)} %bitcast.264), channel_id=1, source_target_pairs={{0,7},{1,0},{2,1},{3,2},{4,3},{5,4},{6,5},{7,6},{8,15},{9,8},{10,9... | collective-permute-start | bytes 104 | tf_op jit(solution)/shard_map/ppermute | solution.py:21
  125.0 6.3 %collective-permute-start.29 = (f32[2,4]{1,0:T(2,128)S(1)}, f32[2,4]{1,0:T(2,128)S(1)}, u32[]{:S(2)}, u32[]{:S(2)}) collective-permute-start(f32[2,4]{1,0:T(2,128)S(1)} %collective-permute-done.27), channel_id=1, source_target_pairs={{0,1},{1,2},{2,3},{3,4},{4,5},{5,6},{6,7},{7,0},{8,9},{9,10},{10,1... | collective-permute-start | bytes 104 | tf_op jit(solution)/shard_map/ppermute | solution.py:18
  125.0 6.3 %collective-permute-start.30 = (f32[2,4]{1,0:T(2,128)S(1)}, f32[2,4]{1,0:T(2,128)S(1)}, u32[]{:S(2)}, u32[]{:S(2)}) collective-permute-start(f32[2,4]{1,0:T(2,128)S(1)} %collective-permute-done.28), channel_id=1, source_target_pairs={{0,7},{1,0},{2,1},{3,2},{4,3},{5,4},{6,5},{7,6},{8,15},{9,8},{10,9... | collective-permute-start | bytes 104 | tf_op jit(solution)/shard_map/ppermute | solution.py:21
  131.2 6.3 %collective-permute-start.31 = (f32[2,4]{1,0:T(2,128)S(1)}, f32[2,4]{1,0:T(2,128)S(1)}, u32[]{:S(2)}, u32[]{:S(2)}) collective-permute-start(f32[2,4]{1,0:T(2,128)S(1)} %collective-permute-done.29), channel_id=1, source_target_pairs={{0,1},{1,2},{2,3},{3,4},{4,5},{5,6},{6,7},{7,0},{8,9},{9,10},{10,1... | collective-permute-start | bytes 104 | tf_op jit(solution)/shard_map/ppermute | solution.py:18
  131.3 6.3 %collective-permute-start.32 = (f32[2,4]{1,0:T(2,128)S(1)}, f32[2,4]{1,0:T(2,128)S(1)}, u32[]{:S(2)}, u32[]{:S(2)}) collective-permute-start(f32[2,4]{1,0:T(2,128)S(1)} %collective-permute-done.30), channel_id=1, source_target_pairs={{0,7},{1,0},{2,1},{3,2},{4,3},{5,4},{6,5},{7,6},{8,15},{9,8},{10,9... | collective-permute-start | bytes 104 | tf_op jit(solution)/shard_map/ppermute | solution.py:21
  137.5 6.3 %collective-permute-start.33 = (f32[2,4]{1,0:T(2,128)S(1)}, f32[2,4]{1,0:T(2,128)S(1)}, u32[]{:S(2)}, u32[]{:S(2)}) collective-permute-start(f32[2,4]{1,0:T(2,128)S(1)} %collective-permute-done.31), channel_id=1, source_target_pairs={{0,1},{1,2},{2,3},{3,4},{4,5},{5,6},{6,7},{7,0},{8,9},{9,10},{10,1... | collective-permute-start | bytes 104 | tf_op jit(solution)/shard_map/ppermute | solution.py:18
  144.3 6.5 %collective-permute-start.36 = (f32[1,2,4,64]{3,2,1,0:T(4,128)S(1)}, f32[1,2,4,64]{3,2,1,0:T(4,128)S(1)}, u32[]{:S(2)}, u32[]{:S(2)}) collective-permute-start(f32[1,2,4,64]{3,2,1,0:T(4,128)S(1)} %get-tuple-element.57), channel_id=1, source_target_pairs={{0,8},{8,16},{16,24},{24,0},{1,9},{9,17},{17,25},{25,1},{2,10},{10... | collective-permute-start | bytes 6152 | tf_op jit(solution)/shard_map/ppermute | solution.py:35
  144.3 8.0 %collective-permute-start.37 = (f32[1,2,4,64]{3,2,1,0:T(4,128)S(1)}, f32[1,2,4,64]{3,2,1,0:T(4,128)S(1)}, u32[]{:S(2)}, u32[]{:S(2)}) collective-permute-start(f32[1,2,4,64]{3,2,1,0:T(4,128)S(1)} %get-tuple-element.57), channel_id=1, source_target_pairs={{8,0},{16,8},{24,16},{0,24},{9,1},{17,9},{25,17},{1,25},{10,2},{18... | collective-permute-start | bytes 6152 | tf_op jit(solution)/shard_map/ppermute | solution.py:37
  146.1 6.3 %collective-permute-start.34 = (f32[1,1,4,64]{3,2,1,0:T(4,128)S(1)}, f32[1,1,4,64]{3,2,1,0:T(4,128)S(1)}, u32[]{:S(2)}, u32[]{:S(2)}) collective-permute-start(f32[1,1,4,64]{3,2,1,0:T(4,128)S(1)} %get-tuple-element.59), channel_id=1, source_target_pairs={{0,1},{1,2},{2,3},{3,4},{4,5},{5,6},{6,7},{7,0},{8,9},{9,10},{10,1... | collective-permute-start | bytes 3080 | tf_op jit(solution)/shard_map/ppermute | solution.py:35
  146.1 6.3 %collective-permute-start.35 = (f32[1,1,4,64]{3,2,1,0:T(4,128)S(1)}, f32[1,1,4,64]{3,2,1,0:T(4,128)S(1)}, u32[]{:S(2)}, u32[]{:S(2)}) collective-permute-start(f32[1,1,4,64]{3,2,1,0:T(4,128)S(1)} %get-tuple-element.60), channel_id=1, source_target_pairs={{1,0},{2,1},{3,2},{4,3},{5,4},{6,5},{7,6},{0,7},{9,8},{10,9},{11,1... | collective-permute-start | bytes 3080 | tf_op jit(solution)/shard_map/ppermute | solution.py:37
  202.6 6.5 %collective-permute-start.40 = (f32[1,2,4,64]{3,2,1,0:T(4,128)S(1)}, f32[1,2,4,64]{3,2,1,0:T(4,128)S(1)}, u32[]{:S(2)}, u32[]{:S(2)}) collective-permute-start(f32[1,2,4,64]{3,2,1,0:T(4,128)S(1)} %get-tuple-element.53), channel_id=1, source_target_pairs={{0,8},{8,16},{16,24},{24,0},{1,9},{9,17},{17,25},{25,1},{2,10},{10... | collective-permute-start | bytes 6152 | tf_op jit(solution)/shard_map/ppermute | solution.py:35
  202.6 8.0 %collective-permute-start.41 = (f32[1,2,4,64]{3,2,1,0:T(4,128)S(1)}, f32[1,2,4,64]{3,2,1,0:T(4,128)S(1)}, u32[]{:S(2)}, u32[]{:S(2)}) collective-permute-start(f32[1,2,4,64]{3,2,1,0:T(4,128)S(1)} %get-tuple-element.53), channel_id=1, source_target_pairs={{8,0},{16,8},{24,16},{0,24},{9,1},{17,9},{25,17},{1,25},{10,2},{18... | collective-permute-start | bytes 6152 | tf_op jit(solution)/shard_map/ppermute | solution.py:37
  204.4 6.3 %collective-permute-start.38 = (f32[1,1,4,64]{3,2,1,0:T(4,128)S(1)}, f32[1,1,4,64]{3,2,1,0:T(4,128)S(1)}, u32[]{:S(2)}, u32[]{:S(2)}) collective-permute-start(f32[1,1,4,64]{3,2,1,0:T(4,128)S(1)} %get-tuple-element.55), channel_id=1, source_target_pairs={{0,1},{1,2},{2,3},{3,4},{4,5},{5,6},{6,7},{7,0},{8,9},{9,10},{10,1... | collective-permute-start | bytes 3080 | tf_op jit(solution)/shard_map/ppermute | solution.py:35
  220.7 6.5 %collective-permute-start.44 = (f32[1,2,4,64]{3,2,1,0:T(4,128)S(1)}, f32[1,2,4,64]{3,2,1,0:T(4,128)S(1)}, u32[]{:S(2)}, u32[]{:S(2)}) collective-permute-start(f32[1,2,4,64]{3,2,1,0:T(4,128)S(1)} %get-tuple-element.49), channel_id=1, source_target_pairs={{0,8},{8,16},{16,24},{24,0},{1,9},{9,17},{17,25},{25,1},{2,10},{10... | collective-permute-start | bytes 6152 | tf_op jit(solution)/shard_map/ppermute | solution.py:35
  220.7 8.0 %collective-permute-start.45 = (f32[1,2,4,64]{3,2,1,0:T(4,128)S(1)}, f32[1,2,4,64]{3,2,1,0:T(4,128)S(1)}, u32[]{:S(2)}, u32[]{:S(2)}) collective-permute-start(f32[1,2,4,64]{3,2,1,0:T(4,128)S(1)} %get-tuple-element.49), channel_id=1, source_target_pairs={{8,0},{16,8},{24,16},{0,24},{9,1},{17,9},{25,17},{1,25},{10,2},{18... | collective-permute-start | bytes 6152 | tf_op jit(solution)/shard_map/ppermute | solution.py:37
  222.5 6.3 %collective-permute-start.42 = (f32[1,1,4,64]{3,2,1,0:T(4,128)S(1)}, f32[1,1,4,64]{3,2,1,0:T(4,128)S(1)}, u32[]{:S(2)}, u32[]{:S(2)}) collective-permute-start(f32[1,1,4,64]{3,2,1,0:T(4,128)S(1)} %get-tuple-element.51), channel_id=1, source_target_pairs={{0,1},{1,2},{2,3},{3,4},{4,5},{5,6},{6,7},{7,0},{8,9},{9,10},{10,1... | collective-permute-start | bytes 3080 | tf_op jit(solution)/shard_map/ppermute | solution.py:35
  238.5 6.5 %collective-permute-start.48 = (f32[1,2,4,64]{3,2,1,0:T(4,128)S(1)}, f32[1,2,4,64]{3,2,1,0:T(4,128)S(1)}, u32[]{:S(2)}, u32[]{:S(2)}) collective-permute-start(f32[1,2,4,64]{3,2,1,0:T(4,128)S(1)} %get-tuple-element.45), channel_id=1, source_target_pairs={{0,8},{8,16},{16,24},{24,0},{1,9},{9,17},{17,25},{25,1},{2,10},{10... | collective-permute-start | bytes 6152 | tf_op jit(solution)/shard_map/ppermute | solution.py:35
  238.6 8.0 %collective-permute-start.49 = (f32[1,2,4,64]{3,2,1,0:T(4,128)S(1)}, f32[1,2,4,64]{3,2,1,0:T(4,128)S(1)}, u32[]{:S(2)}, u32[]{:S(2)}) collective-permute-start(f32[1,2,4,64]{3,2,1,0:T(4,128)S(1)} %get-tuple-element.45), channel_id=1, source_target_pairs={{8,0},{16,8},{24,16},{0,24},{9,1},{17,9},{25,17},{1,25},{10,2},{18... | collective-permute-start | bytes 6152 | tf_op jit(solution)/shard_map/ppermute | solution.py:37
  240.3 6.3 %collective-permute-start.46 = (f32[1,1,4,64]{3,2,1,0:T(4,128)S(1)}, f32[1,1,4,64]{3,2,1,0:T(4,128)S(1)}, u32[]{:S(2)}, u32[]{:S(2)}) collective-permute-start(f32[1,1,4,64]{3,2,1,0:T(4,128)S(1)} %get-tuple-element.47), channel_id=1, source_target_pairs={{0,1},{1,2},{2,3},{3,4},{4,5},{5,6},{6,7},{7,0},{8,9},{9,10},{10,1... | collective-permute-start | bytes 3080 | tf_op jit(solution)/shard_map/ppermute | solution.py:35
  256.4 6.3 %collective-permute-start.50 = (f32[2,4]{1,0:T(2,128)S(1)}, f32[2,4]{1,0:T(2,128)S(1)}, u32[]{:S(2)}, u32[]{:S(2)}) collective-permute-start(f32[2,4]{1,0:T(2,128)S(1)} %bitcast.266), channel_id=1, source_target_pairs={{0,1},{1,2},{2,3},{3,4},{4,5},{5,6},{6,7},{7,0},{8,9},{9,10},{10,1... | collective-permute-start | bytes 104 | tf_op jit(solution)/shard_map/ppermute | solution.py:18
  262.7 6.3 %collective-permute-start.52 = (f32[2,4]{1,0:T(2,128)S(1)}, f32[2,4]{1,0:T(2,128)S(1)}, u32[]{:S(2)}, u32[]{:S(2)}) collective-permute-start(f32[2,4]{1,0:T(2,128)S(1)} %collective-permute-done.50), channel_id=1, source_target_pairs={{0,1},{1,2},{2,3},{3,4},{4,5},{5,6},{6,7},{7,0},{8,9},{9,10},{10,1... | collective-permute-start | bytes 104 | tf_op jit(solution)/shard_map/ppermute | solution.py:18
  269.0 6.3 %collective-permute-start.54 = (f32[2,4]{1,0:T(2,128)S(1)}, f32[2,4]{1,0:T(2,128)S(1)}, u32[]{:S(2)}, u32[]{:S(2)}) collective-permute-start(f32[2,4]{1,0:T(2,128)S(1)} %collective-permute-done.52), channel_id=1, source_target_pairs={{0,1},{1,2},{2,3},{3,4},{4,5},{5,6},{6,7},{7,0},{8,9},{9,10},{10,1... | collective-permute-start | bytes 104 | tf_op jit(solution)/shard_map/ppermute | solution.py:18
  275.2 6.3 %collective-permute-start.56 = (f32[2,4]{1,0:T(2,128)S(1)}, f32[2,4]{1,0:T(2,128)S(1)}, u32[]{:S(2)}, u32[]{:S(2)}) collective-permute-start(f32[2,4]{1,0:T(2,128)S(1)} %collective-permute-done.54), channel_id=1, source_target_pairs={{0,1},{1,2},{2,3},{3,4},{4,5},{5,6},{6,7},{7,0},{8,9},{9,10},{10,1... | collective-permute-start | bytes 104 | tf_op jit(solution)/shard_map/ppermute | solution.py:18
  282.0 6.5 %collective-permute-start.59 = (f32[1,2,4,64]{3,2,1,0:T(4,128)S(1)}, f32[1,2,4,64]{3,2,1,0:T(4,128)S(1)}, u32[]{:S(2)}, u32[]{:S(2)}) collective-permute-start(f32[1,2,4,64]{3,2,1,0:T(4,128)S(1)} %get-tuple-element.41), channel_id=1, source_target_pairs={{0,8},{8,16},{16,24},{24,0},{1,9},{9,17},{17,25},{25,1},{2,10},{10... | collective-permute-start | bytes 6152 | tf_op jit(solution)/shard_map/ppermute | solution.py:35
  282.1 8.0 %collective-permute-start.60 = (f32[1,2,4,64]{3,2,1,0:T(4,128)S(1)}, f32[1,2,4,64]{3,2,1,0:T(4,128)S(1)}, u32[]{:S(2)}, u32[]{:S(2)}) collective-permute-start(f32[1,2,4,64]{3,2,1,0:T(4,128)S(1)} %get-tuple-element.41), channel_id=1, source_target_pairs={{8,0},{16,8},{24,16},{0,24},{9,1},{17,9},{25,17},{1,25},{10,2},{18... | collective-permute-start | bytes 6152 | tf_op jit(solution)/shard_map/ppermute | solution.py:37
  283.8 6.3 %collective-permute-start.57 = (f32[1,1,4,64]{3,2,1,0:T(4,128)S(1)}, f32[1,1,4,64]{3,2,1,0:T(4,128)S(1)}, u32[]{:S(2)}, u32[]{:S(2)}) collective-permute-start(f32[1,1,4,64]{3,2,1,0:T(4,128)S(1)} %get-tuple-element.43), channel_id=1, source_target_pairs={{0,1},{1,2},{2,3},{3,4},{4,5},{5,6},{6,7},{7,0},{8,9},{9,10},{10,1... | collective-permute-start | bytes 3080 | tf_op jit(solution)/shard_map/ppermute | solution.py:35
  283.8 6.3 %collective-permute-start.58 = (f32[1,1,4,64]{3,2,1,0:T(4,128)S(1)}, f32[1,1,4,64]{3,2,1,0:T(4,128)S(1)}, u32[]{:S(2)}, u32[]{:S(2)}) collective-permute-start(f32[1,1,4,64]{3,2,1,0:T(4,128)S(1)} %get-tuple-element.44), channel_id=1, source_target_pairs={{1,0},{2,1},{3,2},{4,3},{5,4},{6,5},{7,6},{0,7},{9,8},{10,9},{11,1... | collective-permute-start | bytes 3080 | tf_op jit(solution)/shard_map/ppermute | solution.py:37
  340.9 6.5 %collective-permute-start.63 = (f32[1,2,4,64]{3,2,1,0:T(4,128)S(1)}, f32[1,2,4,64]{3,2,1,0:T(4,128)S(1)}, u32[]{:S(2)}, u32[]{:S(2)}) collective-permute-start(f32[1,2,4,64]{3,2,1,0:T(4,128)S(1)} %get-tuple-element.37), channel_id=1, source_target_pairs={{0,8},{8,16},{16,24},{24,0},{1,9},{9,17},{17,25},{25,1},{2,10},{10... | collective-permute-start | bytes 6152 | tf_op jit(solution)/shard_map/ppermute | solution.py:35
  340.9 8.0 %collective-permute-start.64 = (f32[1,2,4,64]{3,2,1,0:T(4,128)S(1)}, f32[1,2,4,64]{3,2,1,0:T(4,128)S(1)}, u32[]{:S(2)}, u32[]{:S(2)}) collective-permute-start(f32[1,2,4,64]{3,2,1,0:T(4,128)S(1)} %get-tuple-element.37), channel_id=1, source_target_pairs={{8,0},{16,8},{24,16},{0,24},{9,1},{17,9},{25,17},{1,25},{10,2},{18... | collective-permute-start | bytes 6152 | tf_op jit(solution)/shard_map/ppermute | solution.py:37
  342.7 6.3 %collective-permute-start.61 = (f32[1,1,4,64]{3,2,1,0:T(4,128)S(1)}, f32[1,1,4,64]{3,2,1,0:T(4,128)S(1)}, u32[]{:S(2)}, u32[]{:S(2)}) collective-permute-start(f32[1,1,4,64]{3,2,1,0:T(4,128)S(1)} %get-tuple-element.39), channel_id=1, source_target_pairs={{0,1},{1,2},{2,3},{3,4},{4,5},{5,6},{6,7},{7,0},{8,9},{9,10},{10,1... | collective-permute-start | bytes 3080 | tf_op jit(solution)/shard_map/ppermute | solution.py:35
  359.1 6.5 %collective-permute-start.67 = (f32[1,2,4,64]{3,2,1,0:T(4,128)S(1)}, f32[1,2,4,64]{3,2,1,0:T(4,128)S(1)}, u32[]{:S(2)}, u32[]{:S(2)}) collective-permute-start(f32[1,2,4,64]{3,2,1,0:T(4,128)S(1)} %get-tuple-element.33), channel_id=1, source_target_pairs={{0,8},{8,16},{16,24},{24,0},{1,9},{9,17},{17,25},{25,1},{2,10},{10... | collective-permute-start | bytes 6152 | tf_op jit(solution)/shard_map/ppermute | solution.py:35
  359.1 8.0 %collective-permute-start.68 = (f32[1,2,4,64]{3,2,1,0:T(4,128)S(1)}, f32[1,2,4,64]{3,2,1,0:T(4,128)S(1)}, u32[]{:S(2)}, u32[]{:S(2)}) collective-permute-start(f32[1,2,4,64]{3,2,1,0:T(4,128)S(1)} %get-tuple-element.33), channel_id=1, source_target_pairs={{8,0},{16,8},{24,16},{0,24},{9,1},{17,9},{25,17},{1,25},{10,2},{18... | collective-permute-start | bytes 6152 | tf_op jit(solution)/shard_map/ppermute | solution.py:37
  360.8 6.3 %collective-permute-start.65 = (f32[1,1,4,64]{3,2,1,0:T(4,128)S(1)}, f32[1,1,4,64]{3,2,1,0:T(4,128)S(1)}, u32[]{:S(2)}, u32[]{:S(2)}) collective-permute-start(f32[1,1,4,64]{3,2,1,0:T(4,128)S(1)} %get-tuple-element.35), channel_id=1, source_target_pairs={{0,1},{1,2},{2,3},{3,4},{4,5},{5,6},{6,7},{7,0},{8,9},{9,10},{10,1... | collective-permute-start | bytes 3080 | tf_op jit(solution)/shard_map/ppermute | solution.py:35
  376.9 6.5 %collective-permute-start.71 = (f32[1,2,4,64]{3,2,1,0:T(4,128)S(1)}, f32[1,2,4,64]{3,2,1,0:T(4,128)S(1)}, u32[]{:S(2)}, u32[]{:S(2)}) collective-permute-start(f32[1,2,4,64]{3,2,1,0:T(4,128)S(1)} %get-tuple-element.29), channel_id=1, source_target_pairs={{0,8},{8,16},{16,24},{24,0},{1,9},{9,17},{17,25},{25,1},{2,10},{10... | collective-permute-start | bytes 6152 | tf_op jit(solution)/shard_map/ppermute | solution.py:35
  376.9 8.0 %collective-permute-start.72 = (f32[1,2,4,64]{3,2,1,0:T(4,128)S(1)}, f32[1,2,4,64]{3,2,1,0:T(4,128)S(1)}, u32[]{:S(2)}, u32[]{:S(2)}) collective-permute-start(f32[1,2,4,64]{3,2,1,0:T(4,128)S(1)} %get-tuple-element.29), channel_id=1, source_target_pairs={{8,0},{16,8},{24,16},{0,24},{9,1},{17,9},{25,17},{1,25},{10,2},{18... | collective-permute-start | bytes 6152 | tf_op jit(solution)/shard_map/ppermute | solution.py:37
  378.6 6.3 %collective-permute-start.69 = (f32[1,1,4,64]{3,2,1,0:T(4,128)S(1)}, f32[1,1,4,64]{3,2,1,0:T(4,128)S(1)}, u32[]{:S(2)}, u32[]{:S(2)}) collective-permute-start(f32[1,1,4,64]{3,2,1,0:T(4,128)S(1)} %get-tuple-element.31), channel_id=1, source_target_pairs={{0,1},{1,2},{2,3},{3,4},{4,5},{5,6},{6,7},{7,0},{8,9},{9,10},{10,1... | collective-permute-start | bytes 3080 | tf_op jit(solution)/shard_map/ppermute | solution.py:35
  394.8 6.3 %collective-permute-start.73 = (f32[2,4]{1,0:T(2,128)S(1)}, f32[2,4]{1,0:T(2,128)S(1)}, u32[]{:S(2)}, u32[]{:S(2)}) collective-permute-start(f32[2,4]{1,0:T(2,128)S(1)} %bitcast.260), channel_id=1, source_target_pairs={{0,1},{1,2},{2,3},{3,4},{4,5},{5,6},{6,7},{7,0},{8,9},{9,10},{10,1... | collective-permute-start | bytes 104 | tf_op jit(solution)/shard_map/ppermute | solution.py:18
  401.0 6.3 %collective-permute-start.75 = (f32[2,4]{1,0:T(2,128)S(1)}, f32[2,4]{1,0:T(2,128)S(1)}, u32[]{:S(2)}, u32[]{:S(2)}) collective-permute-start(f32[2,4]{1,0:T(2,128)S(1)} %collective-permute-done.73), channel_id=1, source_target_pairs={{0,1},{1,2},{2,3},{3,4},{4,5},{5,6},{6,7},{7,0},{8,9},{9,10},{10,1... | collective-permute-start | bytes 104 | tf_op jit(solution)/shard_map/ppermute | solution.py:18
  420.4 6.5 %collective-permute-start.82 = (f32[1,2,4,64]{3,2,1,0:T(4,128)S(1)}, f32[1,2,4,64]{3,2,1,0:T(4,128)S(1)}, u32[]{:S(2)}, u32[]{:S(2)}) collective-permute-start(f32[1,2,4,64]{3,2,1,0:T(4,128)S(1)} %get-tuple-element.25), channel_id=1, source_target_pairs={{0,8},{8,16},{16,24},{24,0},{1,9},{9,17},{17,25},{25,1},{2,10},{10... | collective-permute-start | bytes 6152 | tf_op jit(solution)/shard_map/ppermute | solution.py:35
  420.4 8.0 %collective-permute-start.83 = (f32[1,2,4,64]{3,2,1,0:T(4,128)S(1)}, f32[1,2,4,64]{3,2,1,0:T(4,128)S(1)}, u32[]{:S(2)}, u32[]{:S(2)}) collective-permute-start(f32[1,2,4,64]{3,2,1,0:T(4,128)S(1)} %get-tuple-element.25), channel_id=1, source_target_pairs={{8,0},{16,8},{24,16},{0,24},{9,1},{17,9},{25,17},{1,25},{10,2},{18... | collective-permute-start | bytes 6152 | tf_op jit(solution)/shard_map/ppermute | solution.py:37
  422.2 6.3 %collective-permute-start.80 = (f32[1,1,4,64]{3,2,1,0:T(4,128)S(1)}, f32[1,1,4,64]{3,2,1,0:T(4,128)S(1)}, u32[]{:S(2)}, u32[]{:S(2)}) collective-permute-start(f32[1,1,4,64]{3,2,1,0:T(4,128)S(1)} %get-tuple-element.27), channel_id=1, source_target_pairs={{0,1},{1,2},{2,3},{3,4},{4,5},{5,6},{6,7},{7,0},{8,9},{9,10},{10,1... | collective-permute-start | bytes 3080 | tf_op jit(solution)/shard_map/ppermute | solution.py:35
  422.2 6.3 %collective-permute-start.81 = (f32[1,1,4,64]{3,2,1,0:T(4,128)S(1)}, f32[1,1,4,64]{3,2,1,0:T(4,128)S(1)}, u32[]{:S(2)}, u32[]{:S(2)}) collective-permute-start(f32[1,1,4,64]{3,2,1,0:T(4,128)S(1)} %get-tuple-element.28), channel_id=1, source_target_pairs={{1,0},{2,1},{3,2},{4,3},{5,4},{6,5},{7,6},{0,7},{9,8},{10,9},{11,1... | collective-permute-start | bytes 3080 | tf_op jit(solution)/shard_map/ppermute | solution.py:37
  (26 other events, 177.9 us)
